TPU v7x, 32 devices: a whole 2x2x4 slice. The times are simulated.
32 devices in a mesh: data: 2 (over x), pp: 4 (over z), ep: 4 (over y, core).
Axes of the slice: x: 2, y: 2, z: 4, core: 2. Of those that a mesh axis runs over, the one named last changes fastest.
Arguments:
- expert_out: bfloat16 [4, 2, 256, 32, 4096], P('pp', 'data', 'ep'), parts along dimension 1
- expert_ids: int32 [4, 2, 12, 64, 8], P('pp', 'data', 'ep'), parts along dimension 1
- slot_ids: int32 [4, 2, 12, 64, 8], P('pp', 'data', 'ep'), parts along dimension 1
- gate_weights: float32 [4, 2, 12, 64, 8], P('pp', 'data', 'ep'), parts along dimension 1
- residual: bfloat16 [4, 2, 12, 64, 4096], P('pp', 'data', 'ep'), parts along dimension 1
- norm_moe: float32 [4, 4096], P('pp')
- w_gate: bfloat16 [4, 4096, 1024], P('pp')
- w_up: bfloat16 [4, 4096, 1024], P('pp')
- w_down: bfloat16 [4, 1024, 4096], P('pp')
- norm_attn: float32 [4, 4096], P('pp')
- w_query: bfloat16 [4, 4096, 32, 128], P('pp')
- w_key: bfloat16 [4, 4096, 32, 128], P('pp')
- w_value: bfloat16 [4, 4096, 32, 128], P('pp')
- w_out: bfloat16 [4, 32, 128, 4096], P('pp')
Outputs:
- output: bfloat16 [4, 2, 12, 64, 4096], P('pp', 'data', 'ep'), parts along dimension 1
There are 2 independent parts. A program takes and returns all parts, laid end to end along the dimension named above; an argument that names none is the same for every part.
All inputs are finite; a program needn't handle non-finite values.
Results may differ from a plain program's by a relative error of at most 0.0155369.
Values are sent between devices in bfloat16 or wider.
A program may use at most 1 GiB of HBM per device.

v0:
```python
import math
import jax
import jax.numpy as jnp
from jax import lax
from jax.sharding import PartitionSpec as P

EPSILON = 1e-6


def rms_norm(tensor, gain):
    values = tensor.astype(jnp.float32)
    inv_rms = lax.rsqrt(jnp.mean(values * values, axis=-1, keepdims=True) + EPSILON)
    return values * inv_rms * gain


def shared_expert(residual, norm_moe, w_gate, w_up, w_down):
    normed = rms_norm(residual, norm_moe).astype(jnp.bfloat16)
    gate_act = jnp.einsum("bld,df->blf", normed, w_gate, preferred_element_type=jnp.float32)
    up_act = jnp.einsum("bld,df->blf", normed, w_up, preferred_element_type=jnp.float32)
    hidden = (jax.nn.silu(gate_act) * up_act).astype(jnp.bfloat16)
    return jnp.einsum("blf,fd->bld", hidden, w_down, preferred_element_type=jnp.float32).astype(jnp.bfloat16)


def gather_combine(row_table, row_ids, kept_mask, gate_weights):
    picked = jnp.take(row_table, row_ids, axis=0, mode="clip")
    weights = jnp.where(kept_mask, gate_weights, 0.0)
    return jnp.sum(picked.astype(jnp.float32) * weights[..., None], axis=-2)


def attention_block(combined, norm_attn, w_query, w_key, w_value, w_out):
    seq_len = combined.shape[1]
    score_scale = 1.0 / math.sqrt(w_query.shape[2])
    normed = rms_norm(combined, norm_attn).astype(jnp.bfloat16)
    queries = jnp.einsum("bld,dhe->blhe", normed, w_query, preferred_element_type=jnp.float32).astype(jnp.bfloat16)
    key_heads = jnp.einsum("bld,dhe->blhe", normed, w_key, preferred_element_type=jnp.float32).astype(jnp.bfloat16)
    value_heads = jnp.einsum("bld,dhe->blhe", normed, w_value, preferred_element_type=jnp.float32).astype(jnp.bfloat16)
    scores = jnp.einsum("bqhe,bkhe->bhqk", queries, key_heads, preferred_element_type=jnp.float32) * score_scale
    causal = jnp.arange(seq_len)[:, None] >= jnp.arange(seq_len)[None, :]
    scores = jnp.where(causal, scores, -1e30)
    attn_probs = jnp.exp(scores - jnp.max(scores, axis=-1, keepdims=True))
    prob_sum = jnp.sum(attn_probs, axis=-1, keepdims=True)
    attn_mixed = jnp.einsum("bhqk,bkhe->bhqe", attn_probs.astype(jnp.bfloat16), value_heads, preferred_element_type=jnp.float32) / prob_sum
    attn_proj = jnp.einsum("cirf,ife->cre", attn_mixed.astype(jnp.bfloat16), w_out, preferred_element_type=jnp.float32).astype(jnp.bfloat16)
    return (combined.astype(jnp.float32) + attn_proj.astype(jnp.float32)).astype(jnp.bfloat16)


def solution(mesh):
    stages = mesh.shape["pp"]
    ep_size = mesh.shape["ep"]
    shift_pairs = [(source, (source + 1) % stages) for source in range(stages)]
    tok_spec = P("pp", "data", "ep", None, None)
    vec_spec = P("pp", None)
    mat_spec = P("pp", None, None)
    head_spec = P("pp", None, None, None)

    def device_step(expert_out, expert_ids, slot_ids, gate_weights, residual, norm_moe, w_gate, w_up, w_down, norm_attn, w_query, w_key, w_value, w_out):
        micro_count = expert_out.shape[1]
        local_experts, slots_total, model_dim = expert_out.shape[2:]
        cap_slots = slots_total // ep_size
        first_slot = lax.axis_index("ep") * cap_slots
        results = []
        for micro_idx in range(micro_count):
            local_out = expert_out[0, micro_idx].reshape(local_experts, ep_size, cap_slots, model_dim)
            received = lax.all_to_all(local_out, "ep", 1, 0, tiled=True)
            row_table = received.reshape(local_experts * ep_size * cap_slots, model_dim)
            slot_here = slot_ids[0, micro_idx]
            kept_mask = slot_here >= 0
            row_ids = expert_ids[0, micro_idx] * cap_slots + jnp.where(kept_mask, slot_here - first_slot, 0)
            routed = gather_combine(row_table, row_ids, kept_mask, gate_weights[0, micro_idx])
            resid_here = residual[0, micro_idx]
            shared = shared_expert(resid_here, norm_moe[0], w_gate[0], w_up[0], w_down[0])
            combined = (resid_here.astype(jnp.float32) + shared.astype(jnp.float32) + routed).astype(jnp.bfloat16)
            incoming = lax.ppermute(combined, "pp", shift_pairs)
            results.append(attention_block(incoming, norm_attn[0], w_query[0], w_key[0], w_value[0], w_out[0]))
        return jnp.stack(results)[None]

    in_specs = (tok_spec,) * 5 + (vec_spec, mat_spec, mat_spec, mat_spec, vec_spec, head_spec, head_spec, head_spec, head_spec)
    return jax.shard_map(device_step, mesh=mesh, in_specs=in_specs, out_specs=tok_spec, check_vma=False)
```

profile of v0, /device:TPU:0, one launch (start us, length us, event | category | flops | bytes accessed | tf_op | source)
XLA Modules:
  0.0 388.9 jit_solution(11575021855037940030)
XLA Ops:
  0.0 14.0 %copy.17 = bf16[64,4,8,4096]{3,2,0,1:T(8,128)(2,1)} copy(bf16[64,4,8,4096]{3,2,1,0:T(8,128)(2,1)} %bitcast.103) | data formatting | bytes 33554432 | tf_op jit(solution)/shard_map/reshape;squeeze | solution.py:63
  14.0 0.0 copy-start.5
  14.0 7.1 %all-to-all-start = ((bf16[64,4,8,4096]{3,2,0,1:T(8,128)(2,1)}), bf16[64,4,8,4096]{3,2,0,1:T(8,128)(2,1)}, u32[]{:S(2)}, u32[]{:S(2)}) async-start(bf16[64,4,8,4096]{3,2,0,1:T(8,128)(2,1)} %copy.17), calls=%async_computation | async-start | bytes 33554432 | tf_op jit(solution)/shard_map/all_to_all | solution.py:64
  21.1 0.0 copy-done.2
  21.2 0.1 copy.18
  21.3 0.1 reshape.88
  21.4 0.1 copy.19
  21.5 0.4 fusion.49
  21.9 6.1 %fusion.13 = f32[3,64,1024]{2,1,0:T(8,128)} fusion(bf16[1,4096,1024]{2,1,0:T(8,128)(2,1)} %param.20, bf16[1,1,3,64,4096]{4,3,2,1,0:T(8,128)(2,1)S(1)} %copy-done, f32[4096]{0:T(1024)S(1)} %bitcast.107, f32[3,64]{1,0:T(4,128)S(1)} %add_rsqrt_fusion.1), kind=kOutput, calls=%fused_computation.15 | convolution fusion | flops 1613758464 | bytes 10765056 | tf_op jit(solution)/shard_map/bld,df->blf/dot_general | solution.py:18
  28.1 176.5 %all-to-all-done = bf16[64,4,8,4096]{3,2,0,1:T(8,128)(2,1)} async-done(((bf16[64,4,8,4096]{3,2,0,1:T(8,128)(2,1)}), bf16[64,4,8,4096]{3,2,0,1:T(8,128)(2,1)}, u32[]{:S(2)}, u32[]{:S(2)}) %all-to-all-start) | async-done | bytes 16777248 | tf_op jit(solution)/shard_map/all_to_all | solution.py:64
  204.6 30.0 %gather_fusion = bf16[1536,4096]{1,0:T(8,128)(2,1)} fusion(bf16[2048,4096]{1,0:T(8,128)(2,1)} %bitcast.12, s32[2048]{0:T(1024)S(1)} %pad_clamp_fusion), kind=kCustom, calls=%fused_computation | custom fusion | bytes 25171968 | tf_op jit(solution)/shard_map/jit(_take)/gather | solution.py:25
  234.6 12.2 %fusion.8 = f32[3,64,4096]{2,1,0:T(8,128)S(1)} fusion(bf16[3,64,8,4096]{3,2,1,0:T(8,128)(2,1)} %bitcast.102, f32[3,64,8]{2,1,0:T(8,128)S(1)} %copy.19), kind=kLoop, calls=%fused_computation.10 | loop fusion | flops 18087936 | bytes 15734784 | tf_op jit(solution)/shard_map/reduce_sum | solution.py:27
  246.7 0.0 copy-start.6
  246.7 11.6 %fusion.42 = bf16[3,64,4096]{2,1,0:T(8,128)(2,1)} fusion(f32[3,64,4096]{2,1,0:T(8,128)S(1)} %fusion.8, bf16[1,1024,4096]{2,1,0:T(8,128)(2,1)} %param.22, bf16[1,1,3,64,4096]{4,3,2,1,0:T(8,128)(2,1)} %param.18, bf16[1,4096,1024]{2,1,0:T(8,128)(2,1)} %param.21, f32[4096]{0:T(1024)S(1)} %bitcast.108, f32[3,64]{1,0:T(4,128)S(1)} %add_rsqrt_fusion.1, ...), kind=kOutput, calls=%fused_computation.26 | convolution fusion | flops 3230269440 | bytes 23872256 | tf_op jit(solution)/shard_map/blf,fd->bld/dot_general | solution.py:21
  258.3 2.3 collective-permute-start
  260.7 36.7 %collective-permute-done = bf16[3,64,4096]{2,1,0:T(8,128)(2,1)S(1)} collective-permute-done((bf16[3,64,4096]{2,1,0:T(8,128)(2,1)}, bf16[3,64,4096]{2,1,0:T(8,128)(2,1)S(1)}, u32[]{:S(2)}, u32[]{:S(2)}) %collective-permute-start) | collective-permute-done | bytes 1572896 | tf_op jit(solution)/shard_map/ppermute | solution.py:73
  297.3 0.4 fusion.52
  297.8 21.8 %fusion.2 = bf16[3,64,32,128]{3,1,2,0:T(8,128)(2,1)S(1)} fusion(bf16[4096,32,128,1]{2,1,0,3:T(8,128)(2,1)} %bitcast.104, bf16[3,64,4096]{2,1,0:T(8,128)(2,1)S(1)} %collective-permute-done, f32[4096]{0:T(1024)S(1)} %bitcast.109, f32[3,64]{1,0:T(4,128)S(1)} %add_rsqrt_fusion), kind=kOutput, calls=%fused_computation.3 | convolution fusion | flops 6445596672 | bytes 36717312 | tf_op jit(solution)/shard_map/bld,dhe->blhe/dot_general | solution.py:36
  319.6 2.2 copy.41
  321.8 22.8 %fusion.58 = bf16[3,64,32,128]{3,1,2,0:T(8,128)(2,1)} fusion(bf16[4096,32,128,1]{2,1,0,3:T(8,128)(2,1)} %bitcast.105, bf16[3,64,4096]{2,1,0:T(8,128)(2,1)S(1)} %collective-permute-done, f32[4096]{0:T(1024)S(1)} %bitcast.110, f32[3,64]{1,0:T(4,128)S(1)} %add_rsqrt_fusion), kind=kOutput, calls=%fused_computation.46 | convolution fusion | flops 6446383104 | bytes 36717312 | tf_op jit(solution)/shard_map/bld,dhe->blhe/dot_general | solution.py:34
  344.5 22.8 %fusion.61 = bf16[3,64,32,128]{3,1,2,0:T(8,128)(2,1)} fusion(bf16[4096,32,128,1]{2,1,0,3:T(8,128)(2,1)} %bitcast.106, bf16[3,64,4096]{2,1,0:T(8,128)(2,1)S(1)} %collective-permute-done, f32[4096]{0:T(1024)S(1)} %bitcast.111, f32[3,64]{1,0:T(4,128)S(1)} %add_rsqrt_fusion), kind=kOutput, calls=%fused_computation.47 | convolution fusion | flops 6446383104 | bytes 36717312 | tf_op jit(solution)/shard_map/bld,dhe->blhe/dot_general | solution.py:35
  367.3 2.8 fusion.55
  370.2 1.0 fusion.56
  371.2 17.2 %fusion.45 = bf16[1,1,3,64,4096]{4,3,2,1,0:T(8,128)(2,1)} fusion(bf16[1,32,128,4096]{3,2,1,0:T(8,128)(2,1)} %param.27, bf16[3,64,4096]{2,1,0:T(8,128)(2,1)} %copy-done.1, f32[3,32,64,64]{2,3,1,0:T(8,128)S(1)} %get-tuple-element.6, bf16[3,64,32,128]{3,2,1,0:T(8,128)(2,1)} %copy.41, f32[3,32,64]{2,1,0:T(8,128)S(1)} %fusion.56, ...), kind=kOutput, calls=%fused_computation.27 | convolution fusion | flops 6550192128 | bytes 39899136 | tf_op jit(solution)/shard_map/cirf,ife->cre/dot_general | solution.py:43
  (17 shorter events, 0.1 us)
Async XLA Ops:
  14.0 7.1 %copy-start.2 = (s32[1,1,3,64,8]{3,4,2,1,0:T(8,128)S(1)}, s32[1,1,3,64,8]{3,4,2,1,0:T(8,128)}, u32[]{:S(2)}) copy-start(s32[1,1,3,64,8]{3,4,2,1,0:T(8,128)} %param.16) | copy-start | bytes 18436
  14.0 7.1 %copy-start.3 = (s32[1,1,3,64,8]{3,4,2,1,0:T(8,128)S(1)}, s32[1,1,3,64,8]{3,4,2,1,0:T(8,128)}, u32[]{:S(2)}) copy-start(s32[1,1,3,64,8]{3,4,2,1,0:T(8,128)} %param.15) | copy-start | bytes 18436
  14.0 7.4 %copy-start.4 = (f32[1,1,3,64,8]{3,4,2,1,0:T(8,128)S(1)}, f32[1,1,3,64,8]{3,4,2,1,0:T(8,128)}, u32[]{:S(2)}) copy-start(f32[1,1,3,64,8]{3,4,2,1,0:T(8,128)} %param.17) | copy-start | bytes 18436
  14.0 7.5 %copy-start = (bf16[1,1,3,64,4096]{4,3,2,1,0:T(8,128)(2,1)S(1)}, bf16[1,1,3,64,4096]{4,3,2,1,0:T(8,128)(2,1)}, u32[]{:S(2)}) copy-start(bf16[1,1,3,64,4096]{4,3,2,1,0:T(8,128)(2,1)} %param.18) | copy-start | bytes 4718596
  14.0 7.9 %copy-start.5 = (f32[1,4096]{1,0:T(1,128)S(1)}, f32[1,4096]{1,0:T(1,128)}, u32[]{:S(2)}) copy-start(f32[1,4096]{1,0:T(1,128)} %param.19) | copy-start | bytes 49156
  14.0 190.6 %all-to-all-start = ((bf16[64,4,8,4096]{3,2,0,1:T(8,128)(2,1)}), bf16[64,4,8,4096]{3,2,0,1:T(8,128)(2,1)}, u32[]{:S(2)}, u32[]{:S(2)}) async-start(bf16[64,4,8,4096]{3,2,0,1:T(8,128)(2,1)} %copy.17), calls=%async_computation | async-start | bytes 33554432 | tf_op jit(solution)/shard_map/all_to_all | solution.py:64
  246.7 51.0 %copy-start.6 = (f32[1,4096]{1,0:T(1,128)S(1)}, f32[1,4096]{1,0:T(1,128)}, u32[]{:S(2)}) copy-start(f32[1,4096]{1,0:T(1,128)} %param.23) | copy-start | bytes 49156
  258.3 39.0 %collective-permute-start = (bf16[3,64,4096]{2,1,0:T(8,128)(2,1)}, bf16[3,64,4096]{2,1,0:T(8,128)(2,1)S(1)}, u32[]{:S(2)}, u32[]{:S(2)}) collective-permute-start(bf16[3,64,4096]{2,1,0:T(8,128)(2,1)} %fusion.42), channel_id=1, source_target_pairs={{0,4},{4,8},{8,12},{12,0},{1,5},{5,9},{9,13},{13,1},{2,6},{6,10},{... | collective-permute-start | bytes 4718600 | tf_op jit(solution)/shard_map/ppermute | solution.py:73
  297.3 47.2 %copy-start.1 = (bf16[3,64,4096]{2,1,0:T(8,128)(2,1)}, bf16[3,64,4096]{2,1,0:T(8,128)(2,1)S(1)}, u32[]{:S(2)}) copy-start(bf16[3,64,4096]{2,1,0:T(8,128)(2,1)S(1)} %collective-permute-done) | copy-start | bytes 4718596
where the time goes:
time: 397 us; the launch traced here: 389 us
  waiting for transfers between devices  213 us (54%)
  matrix products  105 us (26%)
  local copies, waits for them, and re-layouts  46.4 us (12%)
  other arithmetic  14 us (4%)
  starting transfers between devices  9.43 us (2%)
    all_to_all x1, waiting for transfers between devices, device_step(): received = lax.all_to_all(local_out, 'ep', 1, 0, tiled=True)  177 us
    ppermute x1, waiting for transfers between devices, device_step(): incoming = lax.ppermute(combined, 'pp', shift_pairs)  36.7 us
    gather x1, local copies, waits for them, and re-layouts, gather_combine(): picked = jnp.take(row_table, row_ids, axis=0, mode='clip')  30 us
    dot_general x1, matrix products, attention_block(): jnp.einsum('bld,dhe->blhe', normed, w_key, preferred_element_type=jnp.flo...  22.8 us
    dot_general x1, matrix products, attention_block(): jnp.einsum('bld,dhe->blhe', normed, w_query, preferred_element_type=jnp.f...  22.8 us
    dot_general x1, matrix products, attention_block(): jnp.einsum('bld,dhe->blhe', normed, w_value, preferred_element_type=jnp.f...  21.8 us
    dot_general x1, matrix products, attention_block(): jnp.einsum('cirf,ife->cre', attn_mixed.astype(jnp.bfloat16), w_out, prefe...  17.2 us
    another operation x1, local copies, waits for them, and re-layouts, device_step(): expert_out[0, micro_idx]  14 us
  transfers between devices with their start and end apart: 2, of which 2 were waited for; matrix products, arithmetic and copies ran while one was open for 2% of the time, Pallas kernels for 0%

commit v1 on v0

v1 whole, which is shorter than its diff:
```python
import math
import functools
import jax
import jax.numpy as jnp
from jax import lax
from jax.experimental import pallas as pl
from jax.experimental.pallas import tpu as pltpu
from jax.sharding import PartitionSpec as P

EPSILON = 1e-6
MESH = pl.DeviceIdType.MESH
CHUNK = 32
COLS = 512


def rms_norm(tensor, gain):
    values = tensor.astype(jnp.float32)
    inv_rms = lax.rsqrt(jnp.mean(values * values, axis=-1, keepdims=True) + EPSILON)
    return values * inv_rms * gain


def combine_kernel(
    meta_ref, expert_ref, resid_hbm, norm_ref, gate_hbm, up_hbm, down_hbm, out_ref,
    tab, meta_in, meta_t, pieces, diag_out, diag_in, cross, part_out, part_in, arrive, base,
    resid, normed, hidden, y_out, w_gate, w_up, w_down,
    tab_sem, meta_send, meta_recv, diag_send, diag_recv, part_send, part_recv,
    cross_send, cross_recv, y_send, y_recv, resid_sem, gate_sem, up_sem, down_sem,
):
    tokens, dim = resid.shape
    chunks = tokens // CHUNK
    rows_owner = tab.shape[1] * tab.shape[2]
    slots = tab.shape[2]
    ff_dim = hidden.shape[1]
    me = lax.axis_index("ep")
    stage = lax.axis_index("pp")
    y_pos, core = me // 2, me % 2
    pair = y_pos * 2 + (1 - core)
    across = (1 - y_pos) * 2 + core
    diagonal = (1 - y_pos) * 2 + (1 - core)
    next_stage, prev_stage = (stage + 1) % 4, (stage + 3) % 4

    owners = (diagonal, across, pair, me)

    def table_copy(k):
        start = pl.multiple_of(owners[k] * slots, slots)
        return pltpu.make_async_copy(expert_ref.at[:, pl.ds(start, slots), :], tab.at[k], tab_sem.at[k])

    def resid_copy():
        return pltpu.make_async_copy(resid_hbm, resid, resid_sem)

    ff_tile = w_gate.shape[2]

    def gate_copy(n, slot):
        cols = pl.ds(pl.multiple_of(n * ff_tile, ff_tile), ff_tile)
        return pltpu.make_async_copy(gate_hbm.at[:, cols], w_gate.at[slot], gate_sem.at[slot])

    def up_copy(n, slot):
        cols = pl.ds(pl.multiple_of(n * ff_tile, ff_tile), ff_tile)
        return pltpu.make_async_copy(up_hbm.at[:, cols], w_up.at[slot], up_sem.at[slot])

    def down_copy(n, slot):
        cols = pl.ds(pl.multiple_of(n * COLS, COLS), COLS)
        return pltpu.make_async_copy(down_hbm.at[:, cols], w_down.at[slot], down_sem.at[slot])

    for k in range(4):
        table_copy(k).start()
    resid_copy().start()
    for slot in range(2):
        gate_copy(slot, slot).start()
        up_copy(slot, slot).start()
        down_copy(slot, slot).start()

    barrier = pltpu.get_barrier_semaphore()
    for peer in (pair, across, diagonal):
        pl.semaphore_signal(barrier, inc=1, device_id={"ep": peer}, device_id_type=MESH)
    for peer in (next_stage, prev_stage):
        pl.semaphore_signal(barrier, inc=1, device_id={"pp": peer}, device_id_type=MESH)
    pl.semaphore_wait(barrier, 5)

    def meta_copy(k):
        return pltpu.make_async_remote_copy(
            src_ref=meta_ref, dst_ref=meta_in.at[k], send_sem=meta_send.at[k], recv_sem=meta_recv.at[k],
            device_id={"ep": owners[k]}, device_id_type=MESH)

    for k in range(3):
        meta_copy(k).start()

    def rows_of(c):
        return pl.ds(pl.multiple_of(c * CHUNK, CHUNK), CHUNK)

    def row_copy(src, dst, send, recv, target, c):
        return pltpu.make_async_remote_copy(
            src_ref=src.at[rows_of(c), :], dst_ref=dst.at[rows_of(c), :], send_sem=send.at[c], recv_sem=recv.at[c],
            device_id=target, device_id_type=MESH)

    def diag_copy(c):
        return row_copy(diag_out, diag_in, diag_send, diag_recv, {"ep": pair}, c)

    def part_copy(c):
        return row_copy(part_out, part_in, part_send, part_recv, {"ep": pair}, c)

    def cross_copy(c):
        return row_copy(cross, arrive, cross_send, cross_recv, {"ep": across}, c)

    def y_copy(c):
        return row_copy(y_out, out_ref, y_send, y_recv, {"pp": next_stage}, c)

    def combine(k, c, dst):
        info = meta_t[k, rows_of(c), :]
        col_ids = lax.broadcasted_iota(jnp.int32, (CHUNK, rows_owner), 1) + me * rows_owner
        col_ids = col_ids.astype(jnp.float32)
        weights = jnp.zeros((CHUNK, rows_owner), jnp.float32)
        for j in range(8):
            weights = weights + jnp.where(info[:, j:j + 1] == col_ids, info[:, 8 + j:9 + j], 0.0)
        high = weights.astype(jnp.bfloat16)
        rest = weights - high.astype(jnp.float32)
        middle = rest.astype(jnp.bfloat16)
        rest = rest - middle.astype(jnp.float32)
        pieces[0:CHUNK, :] = high
        pieces[CHUNK:2 * CHUNK, :] = middle
        pieces[2 * CHUNK:3 * CHUNK, :] = rest.astype(jnp.bfloat16)

        def one_tile(n, _):
            cols = pl.ds(pl.multiple_of(n * COLS, COLS), COLS)
            rows = tab[k, :, :, cols].reshape(rows_owner, COLS)
            prod = jnp.dot(pieces[...], rows, preferred_element_type=jnp.float32)
            dst[rows_of(c), cols] = prod[0:CHUNK] + prod[CHUNK:2 * CHUNK] + prod[2 * CHUNK:3 * CHUNK]
            return 0

        lax.fori_loop(0, dim // COLS, one_tile, 0)

    def loop(count, body):
        def step(i, _):
            body(i)
            return 0
        lax.fori_loop(0, count, step, 0)

    meta_t[3] = jnp.transpose(meta_ref[...])
    for k in range(3):
        meta_copy(k).wait_recv()
        meta_t[k] = jnp.transpose(meta_in[k])
    table_copy(0).wait()
    table_copy(1).wait()

    def send_diag(c):
        combine(0, c, diag_out)
        diag_copy(c).start()

    send_diag(0)
    send_diag(1)

    def send_cross(c):
        @pl.when(c + 2 < chunks)
        def _():
            send_diag(c + 2)
        combine(1, c, cross)
        diag_copy(c).wait_recv()
        cross[rows_of(c), :] = cross[rows_of(c), :] + diag_in[rows_of(c), :]
        cross_copy(c).start()

    loop(chunks, send_cross)
    table_copy(2).wait()

    def send_part(c):
        combine(2, c, part_out)
        part_copy(c).start()

    loop(chunks, send_part)
    table_copy(3).wait()
    loop(chunks, lambda c: combine(3, c, base))

    resid_copy().wait()

    def normalize(i):
        rows = pl.ds(pl.multiple_of(i * 16, 16), 16)
        normed[rows, :] = rms_norm(resid[rows, :], norm_ref[...]).astype(jnp.bfloat16)

    loop(tokens // 16, normalize)

    ff_tiles = ff_dim // ff_tile

    def gated(n):
        slot = n % 2
        gate_copy(n, slot).wait()
        up_copy(n, slot).wait()
        gate_act = jnp.dot(normed[...], w_gate[slot], preferred_element_type=jnp.float32)
        up_act = jnp.dot(normed[...], w_up[slot], preferred_element_type=jnp.float32)
        cols = pl.ds(pl.multiple_of(n * ff_tile, ff_tile), ff_tile)
        hidden[:, cols] = (jax.nn.silu(gate_act) * up_act).astype(jnp.bfloat16)

        @pl.when(n + 2 < ff_tiles)
        def _():
            gate_copy(n + 2, slot).start()
            up_copy(n + 2, slot).start()

    loop(ff_tiles, gated)
    loop(chunks, lambda c: part_copy(c).wait_recv())

    def project(n):
        slot = n % 2
        down_copy(n, slot).wait()
        shared = jnp.dot(hidden[...], w_down[slot], preferred_element_type=jnp.float32).astype(jnp.bfloat16)
        cols = pl.ds(pl.multiple_of(n * COLS, COLS), COLS)
        known = resid[:, cols].astype(jnp.float32) + shared.astype(jnp.float32)
        base[:, cols] = known + base[:, cols] + part_in[:, cols]

        @pl.when(n + 2 < dim // COLS)
        def _():
            down_copy(n + 2, slot).start()

    loop(dim // COLS, project)

    def finish(c):
        cross_copy(c).wait_recv()
        y_out[rows_of(c), :] = (base[rows_of(c), :] + arrive[rows_of(c), :]).astype(jnp.bfloat16)
        y_copy(c).start()

    loop(chunks, finish)

    for k in range(3):
        meta_copy(k).wait_send()

    def drain(c):
        diag_copy(c).wait_send()
        part_copy(c).wait_send()
        cross_copy(c).wait_send()
        y_copy(c).wait_send()
        y_copy(c).wait_recv()

    loop(chunks, drain)


def combine_stage(meta, expert_out, resid, norm_moe, w_gate, w_up, w_down):
    tokens, dim = resid.shape
    experts, slots_total, _ = expert_out.shape
    slots = slots_total // 4
    rows_owner = experts * slots
    ff_dim = w_gate.shape[1]
    chunks = tokens // CHUNK
    ff_tile = 256
    f32, bf16 = jnp.float32, jnp.bfloat16
    dma = pltpu.SemaphoreType.DMA
    vmem = pl.BlockSpec(memory_space=pltpu.VMEM)
    hbm = pl.BlockSpec(memory_space=pl.ANY)
    full = (tokens, dim)
    return pl.pallas_call(
        combine_kernel,
        out_shape=jax.ShapeDtypeStruct(full, bf16),
        in_specs=[vmem, hbm, hbm, vmem, hbm, hbm, hbm],
        out_specs=hbm,
        scratch_shapes=[
            pltpu.VMEM((4, experts, slots, dim), bf16),
            pltpu.VMEM((3,) + meta.shape, f32),
            pltpu.VMEM((4, meta.shape[1], meta.shape[0]), f32),
            pltpu.VMEM((3 * CHUNK, rows_owner), bf16),
            pltpu.VMEM(full, f32), pltpu.VMEM(full, f32), pltpu.VMEM(full, f32),
            pltpu.VMEM(full, f32), pltpu.VMEM(full, f32), pltpu.VMEM(full, f32), pltpu.VMEM(full, f32),
            pltpu.VMEM(full, bf16), pltpu.VMEM(full, bf16), pltpu.VMEM((tokens, ff_dim), bf16),
            pltpu.VMEM(full, bf16),
            pltpu.VMEM((2, dim, ff_tile), bf16), pltpu.VMEM((2, dim, ff_tile), bf16),
            pltpu.VMEM((2, ff_dim, COLS), bf16),
            dma((4,)), dma((3,)), dma((3,)),
            dma((chunks,)), dma((chunks,)), dma((chunks,)), dma((chunks,)),
            dma((chunks,)), dma((chunks,)), dma((chunks,)), dma((chunks,)),
            dma(()), dma((2,)), dma((2,)), dma((2,)),
        ],
        compiler_params=pltpu.CompilerParams(
            collective_id=0, has_side_effects=True, vmem_limit_bytes=62 * 1024 * 1024),
        name="combine_stage",
    )(meta, expert_out, resid, norm_moe, w_gate, w_up, w_down)


def attention_block(combined, norm_attn, w_query, w_key, w_value, w_out):
    seq_len = combined.shape[1]
    score_scale = 1.0 / math.sqrt(w_query.shape[2])
    normed = rms_norm(combined, norm_attn).astype(jnp.bfloat16)
    queries = jnp.einsum("bld,dhe->blhe", normed, w_query, preferred_element_type=jnp.float32).astype(jnp.bfloat16)
    key_heads = jnp.einsum("bld,dhe->blhe", normed, w_key, preferred_element_type=jnp.float32).astype(jnp.bfloat16)
    value_heads = jnp.einsum("bld,dhe->blhe", normed, w_value, preferred_element_type=jnp.float32).astype(jnp.bfloat16)
    scores = jnp.einsum("bqhe,bkhe->bhqk", queries, key_heads, preferred_element_type=jnp.float32) * score_scale
    causal = jnp.arange(seq_len)[:, None] >= jnp.arange(seq_len)[None, :]
    scores = jnp.where(causal, scores, -1e30)
    attn_probs = jnp.exp(scores - jnp.max(scores, axis=-1, keepdims=True))
    prob_sum = jnp.sum(attn_probs, axis=-1, keepdims=True)
    attn_mixed = jnp.einsum("bhqk,bkhe->bhqe", attn_probs.astype(jnp.bfloat16), value_heads, preferred_element_type=jnp.float32) / prob_sum
    attn_proj = jnp.einsum("cirf,ife->cre", attn_mixed.astype(jnp.bfloat16), w_out, preferred_element_type=jnp.float32).astype(jnp.bfloat16)
    return (combined.astype(jnp.float32) + attn_proj.astype(jnp.float32)).astype(jnp.bfloat16)


def solution(mesh):
    ep_size = mesh.shape["ep"]
    tok_spec = P("pp", "data", "ep", None, None)
    vec_spec = P("pp", None)
    mat_spec = P("pp", None, None)
    head_spec = P("pp", None, None, None)

    def device_step(expert_out, expert_ids, slot_ids, gate_weights, residual, norm_moe, w_gate, w_up, w_down, norm_attn, w_query, w_key, w_value, w_out):
        seqs, seq_len, top_k = expert_ids.shape[2:]
        tokens = seqs * seq_len
        dim = residual.shape[-1]
        cap_slots = expert_out.shape[3] // ep_size
        first_slot = lax.axis_index("ep") * cap_slots
        slot_here = slot_ids[0, 0]
        kept_mask = slot_here >= 0
        col_ids = jnp.where(kept_mask, expert_ids[0, 0] * cap_slots + slot_here - first_slot, -1)
        weights = jnp.where(kept_mask, gate_weights[0, 0], 0.0)
        meta = jnp.concatenate([col_ids.astype(jnp.float32), weights], axis=-1).reshape(tokens, 2 * top_k)
        meta = jnp.pad(meta.T, ((0, 0), (0, 256 - tokens)))
        incoming = combine_stage(
            meta, expert_out[0, 0], residual.reshape(tokens, dim), norm_moe, w_gate[0], w_up[0], w_down[0])
        incoming = incoming.reshape(seqs, seq_len, dim)
        result = attention_block(incoming, norm_attn[0], w_query[0], w_key[0], w_value[0], w_out[0])
        return result[None, None]

    in_specs = (tok_spec,) * 5 + (vec_spec, mat_spec, mat_spec, mat_spec, vec_spec, head_spec, head_spec, head_spec, head_spec)
    return jax.shard_map(device_step, mesh=mesh, in_specs=in_specs, out_specs=tok_spec, check_vma=False)
```

time: 397 us -> 206 us (0.52); the launches traced: 389 us -> 205 us
  waiting for transfers between devices: 213 us -> 0 us
  Pallas kernels: 0 us -> 106 us
  local copies, waits for them, and re-layouts: 46.4 us -> 4.87 us
  matrix products: 105 us -> 87.9 us
  starting transfers between devices: 9.43 us -> 0 us
  other arithmetic: 14 us -> 6.22 us
    all_to_all x1 -> x0, waiting for transfers between devices: 177 us -> none  [device_step(): received = lax.all_to_all(local_out, 'ep', 1, 0, tiled=True)]
    pallas_call x0 -> x1, Pallas kernels: none -> 106 us  [combine_stage(): pl.pallas_call(combine_kernel, out_shape=jax.ShapeDtypeStruct(full, bf16)...]
    ppermute x1 -> x0, waiting for transfers between devices: 36.7 us -> none  [device_step(): incoming = lax.ppermute(combined, 'pp', shift_pairs)]
    gather x1 -> x0, local copies, waits for them, and re-layouts: 30 us -> none  [gather_combine(): picked = jnp.take(row_table, row_ids, axis=0, mode='clip')]
    dot_general x2 -> x0, matrix products: 17.7 us -> none  [the longest x1 11.6 us: shared_expert(): jnp.einsum('blf,fd->bld', hidden, w_down, preferred_element_type=jnp.floa...]
    another operation x1 -> x0, local copies, waits for them, and re-layouts: 14 us -> none  [device_step(): expert_out[0, micro_idx]]
    reduce_sum x1 -> x0, other arithmetic: 12.2 us -> none  [gather_combine(): return jnp.sum(picked.astype(jnp.float32) * weights[..., None], axis=-2)]
    all_to_all x1 -> x0, starting transfers between devices: 7.1 us -> none  [device_step(): received = lax.all_to_all(local_out, 'ep', 1, 0, tiled=True)]
  transfers between devices with their start and end apart: 2 -> 0, of which waited for: 2 -> 0; matrix products, arithmetic and copies ran while one was open for 2% -> 0% of each run, Pallas kernels for 0% -> 0%
where the time goes in v1:
time: 206 us; the launch traced here: 205 us
  Pallas kernels  106 us (51%)
  matrix products  87.9 us (43%)
  other arithmetic  6.22 us (3%)
  local copies, waits for them, and re-layouts  4.87 us (2%)
    pallas_call x1, Pallas kernels, combine_stage(): pl.pallas_call(combine_kernel, out_shape=jax.ShapeDtypeStruct(full, bf16)...  106 us
    dot_general x1, matrix products, attention_block(): jnp.einsum('bld,dhe->blhe', normed, w_key, preferred_element_type=jnp.flo...  22.8 us
    dot_general x1, matrix products, attention_block(): jnp.einsum('bld,dhe->blhe', normed, w_value, preferred_element_type=jnp.f...  22.6 us
    dot_general x1, matrix products, attention_block(): jnp.einsum('bld,dhe->blhe', normed, w_query, preferred_element_type=jnp.f...  22.5 us
    dot_general x1, matrix products, attention_block(): jnp.einsum('cirf,ife->cre', attn_mixed.astype(jnp.bfloat16), w_out, prefe...  17.2 us

profile of v1, /device:TPU:0, one launch (start us, length us, event | category | flops | bytes accessed | tf_op | source)
XLA Modules:
  0.0 205.2 jit_solution(10243817898317345277)
XLA Ops:
  0.0 0.7 select_convert_fusion
  0.8 0.1 reshape.48
  0.8 0.7 broadcast_select_fusion
  1.6 0.1 select_n.23
  1.7 0.6 pad.4.meta_ref
  2.3 0.0 copy-start.2
  2.3 106.1 %combine_stage.1 = bf16[192,4096]{1,0:T(8,128)(2,1)} custom-call(f32[16,256]{1,0:T(8,128)} %pad.4.meta_ref, bf16[64,32,4096]{2,1,0:T(8,128)(2,1)} %bitcast.61, bf16[192,4096]{1,0:T(8,128)(2,1)} %bitcast.66, f32[1,4096]{1,0:T(1,128)} %norm_ref.1, bf16[4096,1024]{1,0:T(8,128)(2,1)} %bitcast.63, bf16[4096,1024]{1,0:T(8,128)(2,1)} %bitcast.64, ...), custom_call_target="tpu_custom_call" | custom-call | tf_op jit(solution)/shard_map/combine_stage/pallas_call | solution.py:246
  108.4 1.8 multiply_reduce_fusion
  110.2 0.0 copy-done.2
  110.2 1.9 multiply_convert_fusion
  112.1 22.6 %fusion.2 = bf16[3,64,32,128]{3,1,2,0:T(8,128)(2,1)} fusion(bf16[3,64,4096,1]{2,1,3,0:T(8,128)(2,1)S(1)} %bitcast.67, bf16[4096,32,128,1]{2,1,0,3:T(8,128)(2,1)} %bitcast.71), kind=kOutput, calls=%fused_computation.2 | convolution fusion | flops 6442450944 | bytes 36700160 | tf_op jit(solution)/shard_map/bld,dhe->blhe/dot_general | solution.py:279
  134.7 2.4 %copy.40 = bf16[3,64,32,128]{3,2,1,0:T(8,128)(2,1)S(1)} copy(bf16[3,64,32,128]{3,1,2,0:T(8,128)(2,1)} %fusion.2) | data formatting | bytes 3145728 | tf_op jit(solution)/shard_map/bld,dhe->blhe/dot_general | solution.py:279
  137.1 22.8 %fusion.32 = bf16[3,64,32,128]{3,1,2,0:T(8,128)(2,1)} fusion(bf16[3,64,4096,1]{2,1,3,0:T(8,128)(2,1)S(1)} %bitcast.68, bf16[4096,32,128,1]{2,1,0,3:T(8,128)(2,1)} %bitcast.72), kind=kOutput, calls=%fused_computation.24 | convolution fusion | flops 6443237376 | bytes 36700160 | tf_op jit(solution)/shard_map/bld,dhe->blhe/dot_general | solution.py:278
  159.9 22.5 %fusion.29 = bf16[3,64,32,128]{3,1,2,0:T(8,128)(2,1)} fusion(bf16[3,64,4096,1]{2,1,3,0:T(8,128)(2,1)S(1)} %bitcast.69, bf16[4096,32,128,1]{2,1,0,3:T(8,128)(2,1)} %bitcast.73), kind=kOutput, calls=%fused_computation.23 | convolution fusion | flops 6443237376 | bytes 36700160 | tf_op jit(solution)/shard_map/bld,dhe->blhe/dot_general | solution.py:277
  182.4 2.8 %fusion.26 = (f32[3,32,64]{2,1,0:T(8,128)S(1)}, f32[3,32,64,64]{2,3,1,0:T(8,128)S(1)}) fusion(pred[64,64]{0,1:T(8,128)(4,1)S(1)} %iota_compare_fusion, bf16[3,64,32,128]{3,1,2,0:T(8,128)(2,1)} %fusion.29, bf16[3,64,32,128]{3,1,2,0:T(8,128)(2,1)} %fusion.32), kind=kOutput, calls=%fused_computation.20 | convolution fusion | flops 101836800 | bytes 4747264 | tf_op jit(solution)/shard_map/bqhe,bkhe->bhqk/dot_general | solution.py:280
  185.3 0.0 copy-start.1
  185.3 0.0 copy-start
  185.3 1.6 copy-done.1
  186.9 1.0 fusion.27
  188.0 0.0 copy-done
  188.0 17.2 %fusion.23 = bf16[1,1,3,64,4096]{4,3,2,1,0:T(8,128)(2,1)} fusion(bf16[1,32,128,4096]{3,2,1,0:T(8,128)(2,1)} %param.27, f32[3,32,64,64]{2,3,1,0:T(8,128)} %copy-done.1, bf16[3,64,32,128]{3,2,1,0:T(8,128)(2,1)S(1)} %copy.40, f32[3,32,64]{2,1,0:T(8,128)S(1)} %fusion.27, f32[3,32,64]{2,1,0:T(8,128)S(1)} %get-tuple-element.5, ...), kind=kOutput, calls=%fused_computation.13 | convolution fusion | flops 6550192128 | bytes 39899136 | tf_op jit(solution)/shard_map/cirf,ife->cre/dot_general | solution.py:286
  (5 shorter events, 0.0 us)
Async XLA Ops:
  2.3 108.0 %copy-start.2 = (f32[1,4096]{1,0:T(1,128)S(1)}, f32[1,4096]{1,0:T(1,128)}, u32[]{:S(2)}) copy-start(f32[1,4096]{1,0:T(1,128)} %param.23) | copy-start | bytes 49156
  185.3 1.7 copy-start.1
  185.3 2.7 %copy-start = (bf16[192,4096]{1,0:T(8,128)(2,1)S(1)}, bf16[192,4096]{1,0:T(8,128)(2,1)}, u32[]{:S(2)}) copy-start(bf16[192,4096]{1,0:T(8,128)(2,1)} %combine_stage.1) | copy-start | bytes 4718596

commit v2 on v1

--- a/solution.py
+++ b/solution.py
@@ -11,6 +11,7 @@
 MESH = pl.DeviceIdType.MESH
 CHUNK = 32
 COLS = 512
+WIDE = 2048
 
 
 def rms_norm(tensor, gain):
@@ -121,13 +122,13 @@
         pieces[2 * CHUNK:3 * CHUNK, :] = rest.astype(jnp.bfloat16)
 
         def one_tile(n, _):
-            cols = pl.ds(pl.multiple_of(n * COLS, COLS), COLS)
-            rows = tab[k, :, :, cols].reshape(rows_owner, COLS)
+            cols = pl.ds(pl.multiple_of(n * WIDE, WIDE), WIDE)
+            rows = tab[k, :, :, cols].reshape(rows_owner, WIDE)
             prod = jnp.dot(pieces[...], rows, preferred_element_type=jnp.float32)
             dst[rows_of(c), cols] = prod[0:CHUNK] + prod[CHUNK:2 * CHUNK] + prod[2 * CHUNK:3 * CHUNK]
             return 0
 
-        lax.fori_loop(0, dim // COLS, one_tile, 0)
+        lax.fori_loop(0, dim // WIDE, one_tile, 0)
 
     def loop(count, body):
         def step(i, _):
@@ -270,21 +271,132 @@
     )(meta, expert_out, resid, norm_moe, w_gate, w_up, w_down)
 
 
-def attention_block(combined, norm_attn, w_query, w_key, w_value, w_out):
-    seq_len = combined.shape[1]
-    score_scale = 1.0 / math.sqrt(w_query.shape[2])
-    normed = rms_norm(combined, norm_attn).astype(jnp.bfloat16)
-    queries = jnp.einsum("bld,dhe->blhe", normed, w_query, preferred_element_type=jnp.float32).astype(jnp.bfloat16)
-    key_heads = jnp.einsum("bld,dhe->blhe", normed, w_key, preferred_element_type=jnp.float32).astype(jnp.bfloat16)
-    value_heads = jnp.einsum("bld,dhe->blhe", normed, w_value, preferred_element_type=jnp.float32).astype(jnp.bfloat16)
-    scores = jnp.einsum("bqhe,bkhe->bhqk", queries, key_heads, preferred_element_type=jnp.float32) * score_scale
-    causal = jnp.arange(seq_len)[:, None] >= jnp.arange(seq_len)[None, :]
-    scores = jnp.where(causal, scores, -1e30)
-    attn_probs = jnp.exp(scores - jnp.max(scores, axis=-1, keepdims=True))
-    prob_sum = jnp.sum(attn_probs, axis=-1, keepdims=True)
-    attn_mixed = jnp.einsum("bhqk,bkhe->bhqe", attn_probs.astype(jnp.bfloat16), value_heads, preferred_element_type=jnp.float32) / prob_sum
-    attn_proj = jnp.einsum("cirf,ife->cre", attn_mixed.astype(jnp.bfloat16), w_out, preferred_element_type=jnp.float32).astype(jnp.bfloat16)
-    return (combined.astype(jnp.float32) + attn_proj.astype(jnp.float32)).astype(jnp.bfloat16)
+def attention_kernel(
+    seq_len, y_hbm, gain_ref, query_hbm, key_hbm, value_hbm, out_w_hbm, out_hbm,
+    y_in, normed, w_heads, w_cols, heads_qkv, mixed, out_tile,
+    y_sem, head_sem, col_sem, out_sem,
+):
+    tokens, dim = y_in.shape
+    group = w_heads.shape[2]
+    head_dim = w_heads.shape[3]
+    width = group * head_dim
+    groups = mixed.shape[1] // width
+    tile = w_cols.shape[2]
+    weights = (query_hbm, key_hbm, value_hbm)
+
+    def head_copy(g, i):
+        heads = pl.ds(pl.multiple_of(g * group, group), group)
+        return pltpu.make_async_copy(weights[i].at[:, heads, :], w_heads.at[i], head_sem.at[i])
+
+    def col_copy(n, slot):
+        cols = pl.ds(pl.multiple_of(n * tile, tile), tile)
+        return pltpu.make_async_copy(out_w_hbm.at[:, cols], w_cols.at[slot], col_sem.at[slot])
+
+    def out_copy(n, slot):
+        cols = pl.ds(pl.multiple_of(n * tile, tile), tile)
+        return pltpu.make_async_copy(out_tile.at[slot], out_hbm.at[:, cols], out_sem.at[slot])
+
+    def loop(count, body):
+        def step(i, _):
+            body(i)
+            return 0
+        lax.fori_loop(0, count, step, 0)
+
+    y_copy = pltpu.make_async_copy(y_hbm, y_in, y_sem)
+    y_copy.start()
+    head_copy(0, 0).start()
+    head_copy(0, 1).start()
+    y_copy.wait()
+
+    def normalize(i):
+        rows = pl.ds(pl.multiple_of(i * 16, 16), 16)
+        normed[rows, :] = rms_norm(y_in[rows, :], gain_ref[...]).astype(jnp.bfloat16)
+
+    loop(tokens // 16, normalize)
+
+    query_pos = lax.broadcasted_iota(jnp.int32, (tokens, tokens), 0)
+    key_pos = lax.broadcasted_iota(jnp.int32, (tokens, tokens), 1)
+    visible = (query_pos >= key_pos) & (query_pos // seq_len == key_pos // seq_len)
+    score_scale = 1.0 / math.sqrt(head_dim)
+
+    def one_group(g):
+        for i in range(3):
+            head_copy(g, i).wait()
+            if i == 0:
+                head_copy(g, 2).start()
+            else:
+                @pl.when(g + 1 < groups)
+                def _():
+                    head_copy(g + 1, i - 1).start()
+            if i == 2:
+                @pl.when(g == groups - 1)
+                def _():
+                    col_copy(0, 0).start()
+                    col_copy(1, 1).start()
+            flat = w_heads[i].reshape(dim, width)
+            heads_qkv[i] = jnp.dot(normed[...], flat, preferred_element_type=jnp.float32).astype(jnp.bfloat16)
+        for h in range(group):
+            cols = slice(h * head_dim, (h + 1) * head_dim)
+            scores = lax.dot_general(
+                heads_qkv[0, :, cols], heads_qkv[1, :, cols], (((1,), (1,)), ((), ())),
+                preferred_element_type=jnp.float32) * score_scale
+            scores = jnp.where(visible, scores, -1e30)
+            probs = jnp.exp(scores - jnp.max(scores, axis=-1, keepdims=True))
+            prob_sum = jnp.sum(probs, axis=-1, keepdims=True)
+            head_out = jnp.dot(
+                probs.astype(jnp.bfloat16), heads_qkv[2, :, cols], preferred_element_type=jnp.float32) / prob_sum
+            start = pl.multiple_of(g * width + h * head_dim, head_dim)
+            mixed[:, pl.ds(start, head_dim)] = head_out.astype(jnp.bfloat16)
+
+    loop(groups, one_group)
+
+    tiles = dim // tile
+
+    def project(n):
+        slot = n % 2
+        col_copy(n, slot).wait()
+
+        @pl.when(n >= 2)
+        def _():
+            out_copy(n - 2, slot).wait()
+        proj = jnp.dot(mixed[...], w_cols[slot], preferred_element_type=jnp.float32).astype(jnp.bfloat16)
+        cols = pl.ds(pl.multiple_of(n * tile, tile), tile)
+        out_tile[slot] = (y_in[:, cols].astype(jnp.float32) + proj.astype(jnp.float32)).astype(jnp.bfloat16)
+        out_copy(n, slot).start()
+
+        @pl.when(n + 2 < tiles)
+        def _():
+            col_copy(n + 2, slot).start()
+
+    loop(tiles, project)
+    for n in range(tiles - 2, tiles):
+        out_copy(n, n % 2).wait()
+
+
+def attention_stage(seq_len, incoming, norm_attn, w_query, w_key, w_value, w_out):
+    tokens, dim = incoming.shape
+    heads, head_dim = w_query.shape[1:]
+    group = 8
+    tile = 1024
+    bf16 = jnp.bfloat16
+    dma = pltpu.SemaphoreType.DMA
+    vmem = pl.BlockSpec(memory_space=pltpu.VMEM)
+    hbm = pl.BlockSpec(memory_space=pl.ANY)
+    return pl.pallas_call(
+        functools.partial(attention_kernel, seq_len),
+        out_shape=jax.ShapeDtypeStruct((tokens, dim), bf16),
+        in_specs=[hbm, vmem, hbm, hbm, hbm, hbm],
+        out_specs=hbm,
+        scratch_shapes=[
+            pltpu.VMEM((tokens, dim), bf16), pltpu.VMEM((tokens, dim), bf16),
+            pltpu.VMEM((3, dim, group, head_dim), bf16), pltpu.VMEM((2, heads * head_dim, tile), bf16),
+            pltpu.VMEM((3, tokens, group * head_dim), bf16), pltpu.VMEM((tokens, heads * head_dim), bf16),
+            pltpu.VMEM((2, tokens, tile), bf16),
+            dma(()), dma((3,)), dma((2,)), dma((2,)),
+        ],
+        compiler_params=pltpu.CompilerParams(vmem_limit_bytes=62 * 1024 * 1024),
+        name="attention_stage",
+    )(incoming, norm_attn, w_query, w_key, w_value, w_out.reshape(heads * head_dim, dim))
 
 
 def solution(mesh):
@@ -308,9 +420,8 @@
         meta = jnp.pad(meta.T, ((0, 0), (0, 256 - tokens)))
         incoming = combine_stage(
             meta, expert_out[0, 0], residual.reshape(tokens, dim), norm_moe, w_gate[0], w_up[0], w_down[0])
-        incoming = incoming.reshape(seqs, seq_len, dim)
-        result = attention_block(incoming, norm_attn[0], w_query[0], w_key[0], w_value[0], w_out[0])
-        return result[None, None]
+        result = attention_stage(seq_len, incoming, norm_attn, w_query[0], w_key[0], w_value[0], w_out[0])
+        return result.reshape(1, 1, seqs, seq_len, dim)
 
     in_specs = (tok_spec,) * 5 + (vec_spec, mat_spec, mat_spec, mat_spec, vec_spec, head_spec, head_spec, head_spec, head_spec)
     return jax.shard_map(device_step, mesh=mesh, in_specs=in_specs, out_specs=tok_spec, check_vma=False)

time: 206 us -> 156 us (0.76)
  matrix products: 87.9 us -> 0 us
  Pallas kernels: 106 us -> 152 us
  other arithmetic: 6.22 us -> 1.47 us
  local copies, waits for them, and re-layouts: 4.87 us -> 0.79 us
    dot_general x5 -> x0, matrix products: 87.9 us -> none  [the longest x1 22.8 us: attention_block(): jnp.einsum('bld,dhe->blhe', normed, w_key, preferred_element_type=jnp.flo...]
    pallas_call x0 -> x1, Pallas kernels: none -> 61.6 us  [attention_stage(): pl.pallas_call(functools.partial(attention_kernel, seq_len), out_shape=ja...]
    pallas_call x1, Pallas kernels: 106 us -> 90.9 us  [combine_stage(): pl.pallas_call(combine_kernel, out_shape=jax.ShapeDtypeStruct(full, bf16)...]
    reduce_sum x2 -> x0, other arithmetic: 2.85 us -> none  [the longest x1 1.8 us: rms_norm(): jnp.mean(values * values, axis=-1, keepdims=True) + EPSILON]
    dot_general x1 -> x0, local copies, waits for them, and re-layouts: 2.42 us -> none  [attention_block(): jnp.einsum('bld,dhe->blhe', normed, w_value, preferred_element_type=jnp.f...]
where the time goes in v2:
time: 156 us; the launch traced here: 155 us
  Pallas kernels  152 us (97%)
    pallas_call x1, Pallas kernels, combine_stage(): pl.pallas_call(combine_kernel, out_shape=jax.ShapeDtypeStruct(full, bf16)...  90.9 us
    pallas_call x1, Pallas kernels, attention_stage(): pl.pallas_call(functools.partial(attention_kernel, seq_len), out_shape=ja...  61.6 us

profile of v2, /device:TPU:0, one launch (start us, length us, event | category | flops | bytes accessed | tf_op | source)
XLA Modules:
  0.0 154.9 jit_solution(17069950999150151432)
XLA Ops:
  0.0 0.7 select_convert_fusion
  0.7 0.1 reshape.26
  0.8 0.7 broadcast_select_fusion
  1.6 0.1 select_n.19
  1.7 0.6 pad.4.meta_ref
  2.3 90.9 %combine_stage.1.y_hbm = bf16[192,4096]{1,0:T(8,128)(2,1)} custom-call(f32[16,256]{1,0:T(8,128)} %pad.4.meta_ref, bf16[64,32,4096]{2,1,0:T(8,128)(2,1)} %bitcast.20, bf16[192,4096]{1,0:T(8,128)(2,1)} %bitcast.24, f32[1,4096]{1,0:T(1,128)} %norm_ref.1, bf16[4096,1024]{1,0:T(8,128)(2,1)} %bitcast.21, bf16[4096,1024]{1,0:T(8,128)(2,1)} %bitcast.22, ...), custom_call_target="tpu_custom_call" | custom-call | tf_op jit(solution)/shard_map/combine_stage/pallas_call | solution.py:247
  93.2 61.6 %attention_stage.1 = bf16[192,4096]{1,0:T(8,128)(2,1)} custom-call(bf16[192,4096]{1,0:T(8,128)(2,1)} %combine_stage.1.y_hbm, f32[1,4096]{1,0:T(1,128)} %gain_ref.1, bf16[4096,32,128]{2,1,0:T(8,128)(2,1)} %bitcast.16, bf16[4096,32,128]{2,1,0:T(8,128)(2,1)} %bitcast.17, bf16[4096,32,128]{2,1,0:T(8,128)(2,1)} %bitcast.18, bf16[4096,4096]{1,0:T(8,128)(2,1)} %bitcast.19), custom_call_target="tpu_custom_call" | custom-call | tf_op jit(solution)/shard_map/attention_stage/pallas_call | solution.py:385
  (3 shorter events, 0.0 us)

commit v3 on v2

--- a/solution.py
+++ b/solution.py
@@ -10,6 +10,7 @@
 EPSILON = 1e-6
 MESH = pl.DeviceIdType.MESH
 CHUNK = 32
+PART = 16
 COLS = 512
 WIDE = 2048
 
@@ -23,12 +24,13 @@
 def combine_kernel(
     meta_ref, expert_ref, resid_hbm, norm_ref, gate_hbm, up_hbm, down_hbm, out_ref,
     tab, meta_in, meta_t, pieces, diag_out, diag_in, cross, part_out, part_in, arrive, base,
-    resid, normed, hidden, y_out, w_gate, w_up, w_down,
+    resid, normed, hidden, y_out, y_in, w_gate, w_up, w_down,
     tab_sem, meta_send, meta_recv, diag_send, diag_recv, part_send, part_recv,
-    cross_send, cross_recv, y_send, y_recv, resid_sem, gate_sem, up_sem, down_sem,
+    cross_send, cross_recv, y_send, y_recv, pair_send, pair_recv, keep_sem, resid_sem, gate_sem, up_sem, down_sem,
 ):
     tokens, dim = resid.shape
     chunks = tokens // CHUNK
+    parts = tokens // PART
     rows_owner = tab.shape[1] * tab.shape[2]
     slots = tab.shape[2]
     ff_dim = hidden.shape[1]
@@ -100,11 +102,26 @@
     def part_copy(c):
         return row_copy(part_out, part_in, part_send, part_recv, {"ep": pair}, c)
 
+    def rows_of_part(c):
+        return pl.ds(pl.multiple_of(c * PART, PART), PART)
+
+    def part_row_copy(src, dst, send, recv, target, c):
+        return pltpu.make_async_remote_copy(
+            src_ref=src.at[rows_of_part(c), :], dst_ref=dst.at[rows_of_part(c), :],
+            send_sem=send.at[c], recv_sem=recv.at[c], device_id=target, device_id_type=MESH)
+
     def cross_copy(c):
-        return row_copy(cross, arrive, cross_send, cross_recv, {"ep": across}, c)
+        return part_row_copy(cross, arrive, cross_send, cross_recv, {"ep": across}, c)
 
     def y_copy(c):
-        return row_copy(y_out, out_ref, y_send, y_recv, {"pp": next_stage}, c)
+        return part_row_copy(y_out, y_in, y_send, y_recv, {"pp": next_stage}, c)
+
+    def pair_copy(c):
+        return part_row_copy(y_in, out_ref.at[core], pair_send, pair_recv, {"ep": pair}, c)
+
+    def keep_copy(c):
+        rows = rows_of_part(c)
+        return pltpu.make_async_copy(y_in.at[rows, :], out_ref.at[core, rows, :], keep_sem.at[c])
 
     def combine(k, c, dst):
         info = meta_t[k, rows_of(c), :]
@@ -157,7 +174,8 @@
         combine(1, c, cross)
         diag_copy(c).wait_recv()
         cross[rows_of(c), :] = cross[rows_of(c), :] + diag_in[rows_of(c), :]
-        cross_copy(c).start()
+        for i in range(CHUNK // PART):
+            cross_copy(c * (CHUNK // PART) + i).start()
 
     loop(chunks, send_cross)
     table_copy(2).wait()
@@ -212,11 +230,23 @@
     loop(dim // COLS, project)
 
     def finish(c):
+        rows = rows_of_part(c)
         cross_copy(c).wait_recv()
-        y_out[rows_of(c), :] = (base[rows_of(c), :] + arrive[rows_of(c), :]).astype(jnp.bfloat16)
+        y_out[rows, :] = (base[rows, :] + arrive[rows, :]).astype(jnp.bfloat16)
         y_copy(c).start()
 
-    loop(chunks, finish)
+    def spread(c):
+        y_copy(c).wait_recv()
+        pair_copy(c).start()
+        keep_copy(c).start()
+
+    def finish_and_spread(c):
+        finish(c + 1)
+        spread(c)
+
+    finish(0)
+    loop(parts - 1, finish_and_spread)
+    spread(parts - 1)
 
     for k in range(3):
         meta_copy(k).wait_send()
@@ -224,11 +254,17 @@
     def drain(c):
         diag_copy(c).wait_send()
         part_copy(c).wait_send()
+
+    loop(chunks, drain)
+
+    def drain_parts(c):
         cross_copy(c).wait_send()
         y_copy(c).wait_send()
-        y_copy(c).wait_recv()
-
-    loop(chunks, drain)
+        pair_copy(c).wait_send()
+        pair_copy(c).wait_recv()
+        keep_copy(c).wait()
+
+    loop(parts, drain_parts)
 
 
 def combine_stage(meta, expert_out, resid, norm_moe, w_gate, w_up, w_down):
@@ -238,6 +274,7 @@
     rows_owner = experts * slots
     ff_dim = w_gate.shape[1]
     chunks = tokens // CHUNK
+    parts = tokens // PART
     ff_tile = 256
     f32, bf16 = jnp.float32, jnp.bfloat16
     dma = pltpu.SemaphoreType.DMA
@@ -246,7 +283,7 @@
     full = (tokens, dim)
     return pl.pallas_call(
         combine_kernel,
-        out_shape=jax.ShapeDtypeStruct(full, bf16),
+        out_shape=jax.ShapeDtypeStruct((2,) + full, bf16),
         in_specs=[vmem, hbm, hbm, vmem, hbm, hbm, hbm],
         out_specs=hbm,
         scratch_shapes=[
@@ -257,12 +294,13 @@
             pltpu.VMEM(full, f32), pltpu.VMEM(full, f32), pltpu.VMEM(full, f32),
             pltpu.VMEM(full, f32), pltpu.VMEM(full, f32), pltpu.VMEM(full, f32), pltpu.VMEM(full, f32),
             pltpu.VMEM(full, bf16), pltpu.VMEM(full, bf16), pltpu.VMEM((tokens, ff_dim), bf16),
-            pltpu.VMEM(full, bf16),
+            pltpu.VMEM(full, bf16), pltpu.VMEM(full, bf16),
             pltpu.VMEM((2, dim, ff_tile), bf16), pltpu.VMEM((2, dim, ff_tile), bf16),
             pltpu.VMEM((2, ff_dim, COLS), bf16),
             dma((4,)), dma((3,)), dma((3,)),
             dma((chunks,)), dma((chunks,)), dma((chunks,)), dma((chunks,)),
-            dma((chunks,)), dma((chunks,)), dma((chunks,)), dma((chunks,)),
+            dma((parts,)), dma((parts,)), dma((parts,)), dma((parts,)),
+            dma((parts,)), dma((parts,)), dma((parts,)),
             dma(()), dma((2,)), dma((2,)), dma((2,)),
         ],
         compiler_params=pltpu.CompilerParams(
@@ -273,28 +311,46 @@
 
 def attention_kernel(
     seq_len, y_hbm, gain_ref, query_hbm, key_hbm, value_hbm, out_w_hbm, out_hbm,
-    y_in, normed, w_heads, w_cols, heads_qkv, mixed, out_tile,
-    y_sem, head_sem, col_sem, out_sem,
+    y_in, normed, w_heads, w_cols, heads_qkv, mixed_own, mixed_out, mixed_in, out_tile,
+    y_sem, head_sem, col_sem, out_sem, mixed_send, mixed_recv,
 ):
-    tokens, dim = y_in.shape
-    group = w_heads.shape[2]
-    head_dim = w_heads.shape[3]
+    _, tokens, dim = y_hbm.shape
+    group, head_dim = w_heads.shape[2:]
     width = group * head_dim
-    groups = mixed.shape[1] // width
+    groups = mixed_own.shape[1] // width
+    half = groups * width
     tile = w_cols.shape[2]
+    tiles = dim // tile
     weights = (query_hbm, key_hbm, value_hbm)
+    me = lax.axis_index("ep")
+    core = me % 2
+    pair = (me // 2) * 2 + (1 - core)
 
     def head_copy(g, i):
-        heads = pl.ds(pl.multiple_of(g * group, group), group)
+        heads = pl.ds(pl.multiple_of((core * groups + g) * group, group), group)
         return pltpu.make_async_copy(weights[i].at[:, heads, :], w_heads.at[i], head_sem.at[i])
 
-    def col_copy(n, slot):
+    def col_copies(n, slot):
         cols = pl.ds(pl.multiple_of(n * tile, tile), tile)
-        return pltpu.make_async_copy(out_w_hbm.at[:, cols], w_cols.at[slot], col_sem.at[slot])
+        own = pl.ds(pl.multiple_of(core * half, half), half)
+        other = pl.ds(pl.multiple_of((1 - core) * half, half), half)
+        return (
+            pltpu.make_async_copy(out_w_hbm.at[own, cols], w_cols.at[slot, 0:half], col_sem.at[slot, 0]),
+            pltpu.make_async_copy(out_w_hbm.at[other, cols], w_cols.at[slot, half:2 * half], col_sem.at[slot, 1]))
+
+    def col_start(n, slot):
+        for copy in col_copies(n, slot):
+            copy.start()
 
     def out_copy(n, slot):
         cols = pl.ds(pl.multiple_of(n * tile, tile), tile)
         return pltpu.make_async_copy(out_tile.at[slot], out_hbm.at[:, cols], out_sem.at[slot])
+
+    def mixed_copy(g):
+        cols = pl.ds(g * width, width)
+        return pltpu.make_async_remote_copy(
+            src_ref=mixed_out.at[:, cols], dst_ref=mixed_in.at[:, cols], send_sem=mixed_send.at[g],
+            recv_sem=mixed_recv.at[g], device_id={"ep": pair}, device_id_type=MESH)
 
     def loop(count, body):
         def step(i, _):
@@ -302,82 +358,95 @@
             return 0
         lax.fori_loop(0, count, step, 0)
 
-    y_copy = pltpu.make_async_copy(y_hbm, y_in, y_sem)
-    y_copy.start()
+    y_copies = [pltpu.make_async_copy(y_hbm.at[b], y_in.at[pl.ds(b * tokens, tokens), :], y_sem.at[b]) for b in range(2)]
+    for copy in y_copies:
+        copy.start()
     head_copy(0, 0).start()
     head_copy(0, 1).start()
-    y_copy.wait()
+
+    barrier = pltpu.get_barrier_semaphore()
+    pl.semaphore_signal(barrier, inc=1, device_id={"ep": pair}, device_id_type=MESH)
+    pl.semaphore_wait(barrier, 1)
+
+    for copy in y_copies:
+        copy.wait()
 
     def normalize(i):
         rows = pl.ds(pl.multiple_of(i * 16, 16), 16)
         normed[rows, :] = rms_norm(y_in[rows, :], gain_ref[...]).astype(jnp.bfloat16)
 
-    loop(tokens // 16, normalize)
+    loop(2 * tokens // 16, normalize)
 
     query_pos = lax.broadcasted_iota(jnp.int32, (tokens, tokens), 0)
     key_pos = lax.broadcasted_iota(jnp.int32, (tokens, tokens), 1)
     visible = (query_pos >= key_pos) & (query_pos // seq_len == key_pos // seq_len)
     score_scale = 1.0 / math.sqrt(head_dim)
 
-    def one_group(g):
-        for i in range(3):
-            head_copy(g, i).wait()
-            if i == 0:
-                head_copy(g, 2).start()
-            else:
-                @pl.when(g + 1 < groups)
-                def _():
-                    head_copy(g + 1, i - 1).start()
-            if i == 2:
-                @pl.when(g == groups - 1)
-                def _():
-                    col_copy(0, 0).start()
-                    col_copy(1, 1).start()
-            flat = w_heads[i].reshape(dim, width)
-            heads_qkv[i] = jnp.dot(normed[...], flat, preferred_element_type=jnp.float32).astype(jnp.bfloat16)
+    def attend(g, block, dst):
+        rows = pl.ds(pl.multiple_of(block * tokens, tokens), tokens)
         for h in range(group):
             cols = slice(h * head_dim, (h + 1) * head_dim)
             scores = lax.dot_general(
-                heads_qkv[0, :, cols], heads_qkv[1, :, cols], (((1,), (1,)), ((), ())),
+                heads_qkv[0, rows, cols], heads_qkv[1, rows, cols], (((1,), (1,)), ((), ())),
                 preferred_element_type=jnp.float32) * score_scale
             scores = jnp.where(visible, scores, -1e30)
             probs = jnp.exp(scores - jnp.max(scores, axis=-1, keepdims=True))
             prob_sum = jnp.sum(probs, axis=-1, keepdims=True)
             head_out = jnp.dot(
-                probs.astype(jnp.bfloat16), heads_qkv[2, :, cols], preferred_element_type=jnp.float32) / prob_sum
-            start = pl.multiple_of(g * width + h * head_dim, head_dim)
-            mixed[:, pl.ds(start, head_dim)] = head_out.astype(jnp.bfloat16)
-
-    loop(groups, one_group)
-
-    tiles = dim // tile
+                probs.astype(jnp.bfloat16), heads_qkv[2, rows, cols], preferred_element_type=jnp.float32) / prob_sum
+            dst[:, g * width + h * head_dim:g * width + (h + 1) * head_dim] = head_out.astype(jnp.bfloat16)
+
+    for g in range(groups):
+        for i in range(3):
+            head_copy(g, i).wait()
+            if i == 0:
+                head_copy(g, 2).start()
+            elif g + 1 < groups:
+                head_copy(g + 1, i - 1).start()
+            else:
+                col_start(i - 1, i - 1)
+            flat = w_heads[i].reshape(dim, width)
+            heads_qkv[i] = jnp.dot(normed[...], flat, preferred_element_type=jnp.float32).astype(jnp.bfloat16)
+        attend(g, 1 - core, mixed_out)
+        mixed_copy(g).start()
+        attend(g, core, mixed_own)
+
+    for g in range(groups):
+        mixed_copy(g).wait_recv()
 
     def project(n):
         slot = n % 2
-        col_copy(n, slot).wait()
+        for copy in col_copies(n, slot):
+            copy.wait()
 
         @pl.when(n >= 2)
         def _():
             out_copy(n - 2, slot).wait()
-        proj = jnp.dot(mixed[...], w_cols[slot], preferred_element_type=jnp.float32).astype(jnp.bfloat16)
+        proj = jnp.dot(mixed_own[...], w_cols[slot, 0:half], preferred_element_type=jnp.float32)
+        proj = proj + jnp.dot(mixed_in[...], w_cols[slot, half:2 * half], preferred_element_type=jnp.float32)
+        proj = proj.astype(jnp.bfloat16).astype(jnp.float32)
         cols = pl.ds(pl.multiple_of(n * tile, tile), tile)
-        out_tile[slot] = (y_in[:, cols].astype(jnp.float32) + proj.astype(jnp.float32)).astype(jnp.bfloat16)
+        rows = pl.ds(pl.multiple_of(core * tokens, tokens), tokens)
+        out_tile[slot] = (y_in[rows, cols].astype(jnp.float32) + proj).astype(jnp.bfloat16)
         out_copy(n, slot).start()
 
         @pl.when(n + 2 < tiles)
         def _():
-            col_copy(n + 2, slot).start()
+            col_start(n + 2, slot)
 
     loop(tiles, project)
     for n in range(tiles - 2, tiles):
         out_copy(n, n % 2).wait()
+    for g in range(groups):
+        mixed_copy(g).wait_send()
 
 
 def attention_stage(seq_len, incoming, norm_attn, w_query, w_key, w_value, w_out):
-    tokens, dim = incoming.shape
+    _, tokens, dim = incoming.shape
     heads, head_dim = w_query.shape[1:]
     group = 8
     tile = 1024
+    half = heads * head_dim // 2
     bf16 = jnp.bfloat16
     dma = pltpu.SemaphoreType.DMA
     vmem = pl.BlockSpec(memory_space=pltpu.VMEM)
@@ -388,13 +457,15 @@
         in_specs=[hbm, vmem, hbm, hbm, hbm, hbm],
         out_specs=hbm,
         scratch_shapes=[
-            pltpu.VMEM((tokens, dim), bf16), pltpu.VMEM((tokens, dim), bf16),
+            pltpu.VMEM((2 * tokens, dim), bf16), pltpu.VMEM((2 * tokens, dim), bf16),
             pltpu.VMEM((3, dim, group, head_dim), bf16), pltpu.VMEM((2, heads * head_dim, tile), bf16),
-            pltpu.VMEM((3, tokens, group * head_dim), bf16), pltpu.VMEM((tokens, heads * head_dim), bf16),
+            pltpu.VMEM((3, 2 * tokens, group * head_dim), bf16),
+            pltpu.VMEM((tokens, half), bf16), pltpu.VMEM((tokens, half), bf16), pltpu.VMEM((tokens, half), bf16),
             pltpu.VMEM((2, tokens, tile), bf16),
-            dma(()), dma((3,)), dma((2,)), dma((2,)),
+            dma((2,)), dma((3,)), dma((2, 2)), dma((2,)), dma((heads // group // 2,)), dma((heads // group // 2,)),
         ],
-        compiler_params=pltpu.CompilerParams(vmem_limit_bytes=62 * 1024 * 1024),
+        compiler_params=pltpu.CompilerParams(
+            collective_id=1, has_side_effects=True, vmem_limit_bytes=67_000_000),
         name="attention_stage",
     )(incoming, norm_attn, w_query, w_key, w_value, w_out.reshape(heads * head_dim, dim))
 

time: 156 us -> 142 us (0.910)
  Pallas kernels: 152 us -> 136 us
  local copies, waits for them, and re-layouts: 0.79 us -> 3.5 us
    pallas_call x1, Pallas kernels: 61.6 us -> 47.1 us  [attention_stage(): pl.pallas_call(functools.partial(attention_kernel, seq_len), out_shape=ja...]
    unnamed x0 -> x1, local copies, waits for them, and re-layouts: none -> 2.7 us
    pallas_call x1, Pallas kernels: 90.9 us -> 89.1 us  [combine_stage(): pl.pallas_call(combine_kernel, out_shape=jax.ShapeDtypeStruct((2,) + full...]
where the time goes in v3:
time: 142 us; the launch traced here: 141 us
  Pallas kernels  136 us (96%)
  local copies, waits for them, and re-layouts  3.5 us (2%)
  other arithmetic  1.47 us (1%)
    pallas_call x1, Pallas kernels, combine_stage(): pl.pallas_call(combine_kernel, out_shape=jax.ShapeDtypeStruct((2,) + full...  89.1 us
    pallas_call x1, Pallas kernels, attention_stage(): pl.pallas_call(functools.partial(attention_kernel, seq_len), out_shape=ja...  47.1 us

profile of v3, /device:TPU:0, one launch (start us, length us, event | category | flops | bytes accessed | tf_op | source)
XLA Modules:
  0.0 141.2 jit_solution(8857685728947771414)
XLA Ops:
  0.0 0.7 select_convert_fusion
  0.7 0.1 reshape.26
  0.8 0.7 broadcast_select_fusion
  1.6 0.1 select_n.19
  1.7 0.6 pad.4.meta_ref
  2.3 89.1 %combine_stage.1.y_hbm = bf16[2,192,4096]{2,1,0:T(8,128)(2,1)} custom-call(f32[16,256]{1,0:T(8,128)} %pad.4.meta_ref, bf16[64,32,4096]{2,1,0:T(8,128)(2,1)} %bitcast.20, bf16[192,4096]{1,0:T(8,128)(2,1)} %bitcast.25, f32[1,4096]{1,0:T(1,128)} %norm_ref.1, bf16[4096,1024]{1,0:T(8,128)(2,1)} %bitcast.21, bf16[4096,1024]{1,0:T(8,128)(2,1)} %bitcast.22, ...), custom_call_target="tpu_custom_call" | custom-call | tf_op jit(solution)/shard_map/combine_stage/pallas_call | solution.py:284
  91.4 47.1 %attention_stage.1 = bf16[192,4096]{1,0:T(8,128)(2,1)} custom-call(bf16[2,192,4096]{2,1,0:T(8,128)(2,1)} %combine_stage.1.y_hbm, f32[1,4096]{1,0:T(1,128)} %gain_ref.1, bf16[4096,32,128]{2,1,0:T(8,128)(2,1)} %bitcast.16, bf16[4096,32,128]{2,1,0:T(8,128)(2,1)} %bitcast.17, bf16[4096,32,128]{2,1,0:T(8,128)(2,1)} %bitcast.18, bf16[4096,4096]{1,0:T(8,128)(2,1)} %bitcast.19), custom_call_target="tpu_custom_call" | custom-call | tf_op jit(solution)/shard_map/attention_stage/pallas_call | solution.py:454
  138.5 2.7 %copy.20 = bf16[1,1,3,64,4096]{4,3,2,1,0:T(8,128)(2,1)} copy(bf16[1,1,3,64,4096]{4,3,2,1,0:T(8,128)(2,1)} %bitcast.24) | data formatting | bytes 3145728
  (3 shorter events, 0.0 us)

commit v4 on v3

--- a/solution.py
+++ b/solution.py
@@ -22,11 +22,11 @@
 
 
 def combine_kernel(
-    meta_ref, expert_ref, resid_hbm, norm_ref, gate_hbm, up_hbm, down_hbm, out_ref,
+    meta_ref, expert_ref, resid_hbm, norm_ref, next_norm_ref, gate_hbm, up_hbm, down_hbm, x_ref, y_ref,
     tab, meta_in, meta_t, pieces, diag_out, diag_in, cross, part_out, part_in, arrive, base,
     resid, normed, hidden, y_out, y_in, w_gate, w_up, w_down,
     tab_sem, meta_send, meta_recv, diag_send, diag_recv, part_send, part_recv,
-    cross_send, cross_recv, y_send, y_recv, pair_send, pair_recv, keep_sem, resid_sem, gate_sem, up_sem, down_sem,
+    cross_send, cross_recv, y_send, y_recv, pair_send, pair_recv, keep_sem, keep_y_sem, resid_sem, gate_sem, up_sem, down_sem,
 ):
     tokens, dim = resid.shape
     chunks = tokens // CHUNK
@@ -65,13 +65,8 @@
         cols = pl.ds(pl.multiple_of(n * COLS, COLS), COLS)
         return pltpu.make_async_copy(down_hbm.at[:, cols], w_down.at[slot], down_sem.at[slot])
 
-    for k in range(4):
-        table_copy(k).start()
-    resid_copy().start()
-    for slot in range(2):
-        gate_copy(slot, slot).start()
-        up_copy(slot, slot).start()
-        down_copy(slot, slot).start()
+    table_copy(0).start()
+    table_copy(1).start()
 
     barrier = pltpu.get_barrier_semaphore()
     for peer in (pair, across, diagonal):
@@ -117,11 +112,15 @@
         return part_row_copy(y_out, y_in, y_send, y_recv, {"pp": next_stage}, c)
 
     def pair_copy(c):
-        return part_row_copy(y_in, out_ref.at[core], pair_send, pair_recv, {"ep": pair}, c)
+        return part_row_copy(normed, x_ref.at[core], pair_send, pair_recv, {"ep": pair}, c)
 
     def keep_copy(c):
         rows = rows_of_part(c)
-        return pltpu.make_async_copy(y_in.at[rows, :], out_ref.at[core, rows, :], keep_sem.at[c])
+        return pltpu.make_async_copy(normed.at[rows, :], x_ref.at[core, rows, :], keep_sem.at[c])
+
+    def keep_y_copy(c):
+        rows = rows_of_part(c)
+        return pltpu.make_async_copy(y_in.at[rows, :], y_ref.at[rows, :], keep_y_sem.at[c])
 
     def combine(k, c, dst):
         info = meta_t[k, rows_of(c), :]
@@ -153,25 +152,39 @@
             return 0
         lax.fori_loop(0, count, step, 0)
 
-    meta_t[3] = jnp.transpose(meta_ref[...])
+    seqs = meta_ref.shape[0]
+    seq_len = tokens // seqs
+
+    def keep_meta(k, src):
+        for q in range(seqs):
+            meta_t[k, q * seq_len:(q + 1) * seq_len, :] = jnp.transpose(src[q])[0:seq_len]
+
+    keep_meta(3, meta_ref)
     for k in range(3):
         meta_copy(k).wait_recv()
-        meta_t[k] = jnp.transpose(meta_in[k])
+        keep_meta(k, meta_in.at[k])
     table_copy(0).wait()
+    table_copy(2).start()
     table_copy(1).wait()
+    table_copy(3).start()
+    resid_copy().start()
+    for slot in range(2):
+        gate_copy(slot, slot).start()
+        up_copy(slot, slot).start()
+        down_copy(slot, slot).start()
 
     def send_diag(c):
         combine(0, c, diag_out)
         diag_copy(c).start()
 
     send_diag(0)
-    send_diag(1)
 
     def send_cross(c):
-        @pl.when(c + 2 < chunks)
+        combine(1, c, cross)
+
+        @pl.when(c + 1 < chunks)
         def _():
-            send_diag(c + 2)
-        combine(1, c, cross)
+            send_diag(c + 1)
         diag_copy(c).wait_recv()
         cross[rows_of(c), :] = cross[rows_of(c), :] + diag_in[rows_of(c), :]
         for i in range(CHUNK // PART):
@@ -236,7 +249,10 @@
         y_copy(c).start()
 
     def spread(c):
+        rows = rows_of_part(c)
         y_copy(c).wait_recv()
+        keep_y_copy(c).start()
+        normed[rows, :] = rms_norm(y_in[rows, :], next_norm_ref[...]).astype(jnp.bfloat16)
         pair_copy(c).start()
         keep_copy(c).start()
 
@@ -263,11 +279,12 @@
         pair_copy(c).wait_send()
         pair_copy(c).wait_recv()
         keep_copy(c).wait()
+        keep_y_copy(c).wait()
 
     loop(parts, drain_parts)
 
 
-def combine_stage(meta, expert_out, resid, norm_moe, w_gate, w_up, w_down):
+def combine_stage(meta, expert_out, resid, norm_moe, norm_next, w_gate, w_up, w_down):
     tokens, dim = resid.shape
     experts, slots_total, _ = expert_out.shape
     slots = slots_total // 4
@@ -283,13 +300,13 @@
     full = (tokens, dim)
     return pl.pallas_call(
         combine_kernel,
-        out_shape=jax.ShapeDtypeStruct((2,) + full, bf16),
-        in_specs=[vmem, hbm, hbm, vmem, hbm, hbm, hbm],
-        out_specs=hbm,
+        out_shape=(jax.ShapeDtypeStruct((2,) + full, bf16), jax.ShapeDtypeStruct(full, bf16)),
+        in_specs=[vmem, hbm, hbm, vmem, vmem, hbm, hbm, hbm],
+        out_specs=(hbm, hbm),
         scratch_shapes=[
             pltpu.VMEM((4, experts, slots, dim), bf16),
             pltpu.VMEM((3,) + meta.shape, f32),
-            pltpu.VMEM((4, meta.shape[1], meta.shape[0]), f32),
+            pltpu.VMEM((4, tokens, meta.shape[1]), f32),
             pltpu.VMEM((3 * CHUNK, rows_owner), bf16),
             pltpu.VMEM(full, f32), pltpu.VMEM(full, f32), pltpu.VMEM(full, f32),
             pltpu.VMEM(full, f32), pltpu.VMEM(full, f32), pltpu.VMEM(full, f32), pltpu.VMEM(full, f32),
@@ -300,21 +317,21 @@
             dma((4,)), dma((3,)), dma((3,)),
             dma((chunks,)), dma((chunks,)), dma((chunks,)), dma((chunks,)),
             dma((parts,)), dma((parts,)), dma((parts,)), dma((parts,)),
-            dma((parts,)), dma((parts,)), dma((parts,)),
+            dma((parts,)), dma((parts,)), dma((parts,)), dma((parts,)),
             dma(()), dma((2,)), dma((2,)), dma((2,)),
         ],
         compiler_params=pltpu.CompilerParams(
             collective_id=0, has_side_effects=True, vmem_limit_bytes=62 * 1024 * 1024),
         name="combine_stage",
-    )(meta, expert_out, resid, norm_moe, w_gate, w_up, w_down)
+    )(meta, expert_out, resid, norm_moe, norm_next, w_gate, w_up, w_down)
 
 
 def attention_kernel(
-    seq_len, y_hbm, gain_ref, query_hbm, key_hbm, value_hbm, out_w_hbm, out_hbm,
+    seq_len, x_hbm, y_hbm, query_hbm, key_hbm, value_hbm, out_w_hbm, out_hbm,
     y_in, normed, w_heads, w_cols, heads_qkv, mixed_own, mixed_out, mixed_in, out_tile,
-    y_sem, head_sem, col_sem, out_sem, mixed_send, mixed_recv,
+    x_sem, y_sem, head_sem, col_sem, out_sem, mixed_send, mixed_recv,
 ):
-    _, tokens, dim = y_hbm.shape
+    tokens, dim = y_hbm.shape
     group, head_dim = w_heads.shape[2:]
     width = group * head_dim
     groups = mixed_own.shape[1] // width
@@ -358,24 +375,22 @@
             return 0
         lax.fori_loop(0, count, step, 0)
 
-    y_copies = [pltpu.make_async_copy(y_hbm.at[b], y_in.at[pl.ds(b * tokens, tokens), :], y_sem.at[b]) for b in range(2)]
-    for copy in y_copies:
+    x_copies = [
+        pltpu.make_async_copy(x_hbm.at[b], normed.at[pl.ds(b * tokens, tokens), :], x_sem.at[b]) for b in range(2)]
+    y_copy = pltpu.make_async_copy(y_hbm, y_in, y_sem)
+    for copy in x_copies:
         copy.start()
     head_copy(0, 0).start()
     head_copy(0, 1).start()
+    y_copy.start()
 
     barrier = pltpu.get_barrier_semaphore()
     pl.semaphore_signal(barrier, inc=1, device_id={"ep": pair}, device_id_type=MESH)
     pl.semaphore_wait(barrier, 1)
 
-    for copy in y_copies:
+    for copy in x_copies:
         copy.wait()
-
-    def normalize(i):
-        rows = pl.ds(pl.multiple_of(i * 16, 16), 16)
-        normed[rows, :] = rms_norm(y_in[rows, :], gain_ref[...]).astype(jnp.bfloat16)
-
-    loop(2 * tokens // 16, normalize)
+    y_copy.wait()
 
     query_pos = lax.broadcasted_iota(jnp.int32, (tokens, tokens), 0)
     key_pos = lax.broadcasted_iota(jnp.int32, (tokens, tokens), 1)
@@ -426,8 +441,7 @@
         proj = proj + jnp.dot(mixed_in[...], w_cols[slot, half:2 * half], preferred_element_type=jnp.float32)
         proj = proj.astype(jnp.bfloat16).astype(jnp.float32)
         cols = pl.ds(pl.multiple_of(n * tile, tile), tile)
-        rows = pl.ds(pl.multiple_of(core * tokens, tokens), tokens)
-        out_tile[slot] = (y_in[rows, cols].astype(jnp.float32) + proj).astype(jnp.bfloat16)
+        out_tile[slot] = (y_in[:, cols].astype(jnp.float32) + proj).astype(jnp.bfloat16)
         out_copy(n, slot).start()
 
         @pl.when(n + 2 < tiles)
@@ -441,33 +455,32 @@
         mixed_copy(g).wait_send()
 
 
-def attention_stage(seq_len, incoming, norm_attn, w_query, w_key, w_value, w_out):
-    _, tokens, dim = incoming.shape
+def attention_stage(seq_len, normed, incoming, w_query, w_key, w_value, w_out):
+    tokens, dim = incoming.shape
     heads, head_dim = w_query.shape[1:]
     group = 8
     tile = 1024
     half = heads * head_dim // 2
     bf16 = jnp.bfloat16
     dma = pltpu.SemaphoreType.DMA
-    vmem = pl.BlockSpec(memory_space=pltpu.VMEM)
     hbm = pl.BlockSpec(memory_space=pl.ANY)
     return pl.pallas_call(
         functools.partial(attention_kernel, seq_len),
         out_shape=jax.ShapeDtypeStruct((tokens, dim), bf16),
-        in_specs=[hbm, vmem, hbm, hbm, hbm, hbm],
+        in_specs=[hbm] * 6,
         out_specs=hbm,
         scratch_shapes=[
-            pltpu.VMEM((2 * tokens, dim), bf16), pltpu.VMEM((2 * tokens, dim), bf16),
+            pltpu.VMEM((tokens, dim), bf16), pltpu.VMEM((2 * tokens, dim), bf16),
             pltpu.VMEM((3, dim, group, head_dim), bf16), pltpu.VMEM((2, heads * head_dim, tile), bf16),
             pltpu.VMEM((3, 2 * tokens, group * head_dim), bf16),
             pltpu.VMEM((tokens, half), bf16), pltpu.VMEM((tokens, half), bf16), pltpu.VMEM((tokens, half), bf16),
             pltpu.VMEM((2, tokens, tile), bf16),
-            dma((2,)), dma((3,)), dma((2, 2)), dma((2,)), dma((heads // group // 2,)), dma((heads // group // 2,)),
+            dma((2,)), dma(()), dma((3,)), dma((2, 2)), dma((2,)), dma((heads // group // 2,)), dma((heads // group // 2,)),
         ],
         compiler_params=pltpu.CompilerParams(
             collective_id=1, has_side_effects=True, vmem_limit_bytes=67_000_000),
         name="attention_stage",
-    )(incoming, norm_attn, w_query, w_key, w_value, w_out.reshape(heads * head_dim, dim))
+    )(normed, incoming, w_query, w_key, w_value, w_out.reshape(heads * head_dim, dim))
 
 
 def solution(mesh):
@@ -483,15 +496,19 @@
         dim = residual.shape[-1]
         cap_slots = expert_out.shape[3] // ep_size
         first_slot = lax.axis_index("ep") * cap_slots
-        slot_here = slot_ids[0, 0]
+
+        def choices_first(array):
+            return jnp.swapaxes(array[0, 0], 1, 2)
+
+        slot_here = choices_first(slot_ids)
         kept_mask = slot_here >= 0
-        col_ids = jnp.where(kept_mask, expert_ids[0, 0] * cap_slots + slot_here - first_slot, -1)
-        weights = jnp.where(kept_mask, gate_weights[0, 0], 0.0)
-        meta = jnp.concatenate([col_ids.astype(jnp.float32), weights], axis=-1).reshape(tokens, 2 * top_k)
-        meta = jnp.pad(meta.T, ((0, 0), (0, 256 - tokens)))
-        incoming = combine_stage(
-            meta, expert_out[0, 0], residual.reshape(tokens, dim), norm_moe, w_gate[0], w_up[0], w_down[0])
-        result = attention_stage(seq_len, incoming, norm_attn, w_query[0], w_key[0], w_value[0], w_out[0])
+        col_ids = jnp.where(kept_mask, choices_first(expert_ids) * cap_slots + slot_here - first_slot, -1)
+        weights = jnp.where(kept_mask, choices_first(gate_weights), 0.0)
+        meta = jnp.concatenate([col_ids.astype(jnp.float32), weights], axis=1)
+        meta = jnp.pad(meta, ((0, 0), (0, 0), (0, 128 - seq_len)))
+        normed, incoming = combine_stage(
+            meta, expert_out[0, 0], residual.reshape(tokens, dim), norm_moe, norm_attn, w_gate[0], w_up[0], w_down[0])
+        result = attention_stage(seq_len, normed, incoming, w_query[0], w_key[0], w_value[0], w_out[0])
         return result.reshape(1, 1, seqs, seq_len, dim)
 
     in_specs = (tok_spec,) * 5 + (vec_spec, mat_spec, mat_spec, mat_spec, vec_spec, head_spec, head_spec, head_spec, head_spec)

time: 142 us -> 137 us (0.965)
  Pallas kernels: 136 us -> 132 us
    pallas_call x1, Pallas kernels: 47.1 us -> 43.1 us  [attention_stage(): pl.pallas_call(functools.partial(attention_kernel, seq_len), out_shape=ja...]
where the time goes in v4:
time: 137 us; the launch traced here: 136 us
  Pallas kernels  132 us (96%)
  local copies, waits for them, and re-layouts  2.7 us (2%)
  other arithmetic  2.07 us (2%)
    pallas_call x1, Pallas kernels, combine_stage(): pl.pallas_call(combine_kernel, out_shape=(jax.ShapeDtypeStruct((2,) + ful...  88.5 us
    pallas_call x1, Pallas kernels, attention_stage(): pl.pallas_call(functools.partial(attention_kernel, seq_len), out_shape=ja...  43.1 us

profile of v4, /device:TPU:0, one launch (start us, length us, event | category | flops | bytes accessed | tf_op | source)
XLA Modules:
  0.0 136.3 jit_solution(13336968170748467262)
XLA Ops:
  0.0 0.7 convert_bitcast_fusion
  0.7 0.7 select_bitcast_fusion
  1.5 0.6 select_maximum_fusion.meta_ref
  2.1 88.5 %combine_stage.1 = (bf16[2,192,4096]{2,1,0:T(8,128)(2,1)}, bf16[192,4096]{1,0:T(8,128)(2,1)}) custom-call(f32[3,16,128]{2,1,0:T(8,128)} %select_maximum_fusion.meta_ref, bf16[64,32,4096]{2,1,0:T(8,128)(2,1)} %bitcast.22, bf16[192,4096]{1,0:T(8,128)(2,1)} %bitcast.27, f32[1,4096]{1,0:T(1,128)} %norm_ref.1, f32[1,4096]{1,0:T(1,128)} %next_norm_ref.1, ...), custom_call_target="tpu_custom_call" | custom-call | tf_op jit(solution)/shard_map/combine_stage/pallas_call | solution.py:301
  90.5 43.1 %attention_stage.1 = bf16[192,4096]{1,0:T(8,128)(2,1)} custom-call(bf16[2,192,4096]{2,1,0:T(8,128)(2,1)} %get-tuple-element.7.x_hbm, bf16[192,4096]{1,0:T(8,128)(2,1)} %get-tuple-element.8.y_hbm, bf16[4096,32,128]{2,1,0:T(8,128)(2,1)} %bitcast.18, bf16[4096,32,128]{2,1,0:T(8,128)(2,1)} %bitcast.19, bf16[4096,32,128]{2,1,0:T(8,128)(2,1)} %bitcast.20, ...), custom_call_target="tpu_custom_call" | custom-call | tf_op jit(solution)/shard_map/attention_stage/pallas_call | solution.py:467
  133.6 2.7 %copy.16 = bf16[1,1,3,64,4096]{4,3,2,1,0:T(8,128)(2,1)} copy(bf16[1,1,3,64,4096]{4,3,2,1,0:T(8,128)(2,1)} %bitcast.26) | data formatting | bytes 3145728

commit v5 on v4

--- a/solution.py
+++ b/solution.py
@@ -22,8 +22,8 @@
 
 
 def combine_kernel(
-    meta_ref, expert_ref, resid_hbm, norm_ref, next_norm_ref, gate_hbm, up_hbm, down_hbm, x_ref, y_ref,
-    tab, meta_in, meta_t, pieces, diag_out, diag_in, cross, part_out, part_in, arrive, base,
+    ids_ref, slot_ref, gates_ref, expert_ref, resid_hbm, norm_ref, next_norm_ref, gate_hbm, up_hbm, down_hbm, x_ref, y_ref,
+    tab, meta_ref, meta_in, meta_t, pieces, diag_out, diag_in, cross, part_out, part_in, arrive, base,
     resid, normed, hidden, y_out, y_in, w_gate, w_up, w_down,
     tab_sem, meta_send, meta_recv, diag_send, diag_recv, part_send, part_recv,
     cross_send, cross_recv, y_send, y_recv, pair_send, pair_recv, keep_sem, keep_y_sem, resid_sem, gate_sem, up_sem, down_sem,
@@ -68,6 +68,13 @@
     table_copy(0).start()
     table_copy(1).start()
 
+    seqs, choices, seq_len = ids_ref.shape
+    kept = slot_ref[...] >= 0
+    col_ids_own = jnp.where(kept, ids_ref[...] * slots + slot_ref[...] - me * slots, -1)
+    meta_ref[...] = jnp.zeros_like(meta_ref)
+    meta_ref[:, 0:choices, 0:seq_len] = col_ids_own.astype(jnp.float32)
+    meta_ref[:, choices:2 * choices, 0:seq_len] = jnp.where(kept, gates_ref[...], 0.0)
+
     barrier = pltpu.get_barrier_semaphore()
     for peer in (pair, across, diagonal):
         pl.semaphore_signal(barrier, inc=1, device_id={"ep": peer}, device_id_type=MESH)
@@ -152,9 +159,6 @@
             return 0
         lax.fori_loop(0, count, step, 0)
 
-    seqs = meta_ref.shape[0]
-    seq_len = tokens // seqs
-
     def keep_meta(k, src):
         for q in range(seqs):
             meta_t[k, q * seq_len:(q + 1) * seq_len, :] = jnp.transpose(src[q])[0:seq_len]
@@ -284,7 +288,7 @@
     loop(parts, drain_parts)
 
 
-def combine_stage(meta, expert_out, resid, norm_moe, norm_next, w_gate, w_up, w_down):
+def combine_stage(ids, slot_ids, gates, expert_out, resid, norm_moe, norm_next, w_gate, w_up, w_down):
     tokens, dim = resid.shape
     experts, slots_total, _ = expert_out.shape
     slots = slots_total // 4
@@ -298,15 +302,17 @@
     vmem = pl.BlockSpec(memory_space=pltpu.VMEM)
     hbm = pl.BlockSpec(memory_space=pl.ANY)
     full = (tokens, dim)
+    meta_shape = (ids.shape[0], 2 * ids.shape[1], 128)
     return pl.pallas_call(
         combine_kernel,
         out_shape=(jax.ShapeDtypeStruct((2,) + full, bf16), jax.ShapeDtypeStruct(full, bf16)),
-        in_specs=[vmem, hbm, hbm, vmem, vmem, hbm, hbm, hbm],
+        in_specs=[vmem, vmem, vmem, hbm, hbm, vmem, vmem, hbm, hbm, hbm],
         out_specs=(hbm, hbm),
         scratch_shapes=[
             pltpu.VMEM((4, experts, slots, dim), bf16),
-            pltpu.VMEM((3,) + meta.shape, f32),
-            pltpu.VMEM((4, tokens, meta.shape[1]), f32),
+            pltpu.VMEM(meta_shape, f32),
+            pltpu.VMEM((3,) + meta_shape, f32),
+            pltpu.VMEM((4, tokens, meta_shape[1]), f32),
             pltpu.VMEM((3 * CHUNK, rows_owner), bf16),
             pltpu.VMEM(full, f32), pltpu.VMEM(full, f32), pltpu.VMEM(full, f32),
             pltpu.VMEM(full, f32), pltpu.VMEM(full, f32), pltpu.VMEM(full, f32), pltpu.VMEM(full, f32),
@@ -323,15 +329,15 @@
         compiler_params=pltpu.CompilerParams(
             collective_id=0, has_side_effects=True, vmem_limit_bytes=62 * 1024 * 1024),
         name="combine_stage",
-    )(meta, expert_out, resid, norm_moe, norm_next, w_gate, w_up, w_down)
+    )(ids, slot_ids, gates, expert_out, resid, norm_moe, norm_next, w_gate, w_up, w_down)
 
 
 def attention_kernel(
-    seq_len, x_hbm, y_hbm, query_hbm, key_hbm, value_hbm, out_w_hbm, out_hbm,
-    y_in, normed, w_heads, w_cols, heads_qkv, mixed_own, mixed_out, mixed_in, out_tile,
-    x_sem, y_sem, head_sem, col_sem, out_sem, mixed_send, mixed_recv,
+    seq_len, x_hbm, query_hbm, key_hbm, value_hbm, out_w_hbm, out_hbm,
+    normed, w_heads, w_cols, heads_qkv, mixed_own, mixed_out, mixed_in, out_tile,
+    x_sem, head_sem, col_sem, out_sem, mixed_send, mixed_recv,
 ):
-    tokens, dim = y_hbm.shape
+    _, tokens, dim = x_hbm.shape
     group, head_dim = w_heads.shape[2:]
     width = group * head_dim
     groups = mixed_own.shape[1] // width
@@ -377,12 +383,9 @@
 
     x_copies = [
         pltpu.make_async_copy(x_hbm.at[b], normed.at[pl.ds(b * tokens, tokens), :], x_sem.at[b]) for b in range(2)]
-    y_copy = pltpu.make_async_copy(y_hbm, y_in, y_sem)
     for copy in x_copies:
         copy.start()
     head_copy(0, 0).start()
-    head_copy(0, 1).start()
-    y_copy.start()
 
     barrier = pltpu.get_barrier_semaphore()
     pl.semaphore_signal(barrier, inc=1, device_id={"ep": pair}, device_id_type=MESH)
@@ -390,7 +393,6 @@
 
     for copy in x_copies:
         copy.wait()
-    y_copy.wait()
 
     query_pos = lax.broadcasted_iota(jnp.int32, (tokens, tokens), 0)
     key_pos = lax.broadcasted_iota(jnp.int32, (tokens, tokens), 1)
@@ -414,12 +416,13 @@
     for g in range(groups):
         for i in range(3):
             head_copy(g, i).wait()
-            if i == 0:
-                head_copy(g, 2).start()
+            if i < 2:
+                head_copy(g, i + 1).start()
             elif g + 1 < groups:
-                head_copy(g + 1, i - 1).start()
+                head_copy(g + 1, 0).start()
             else:
-                col_start(i - 1, i - 1)
+                col_start(0, 0)
+                col_start(1, 1)
             flat = w_heads[i].reshape(dim, width)
             heads_qkv[i] = jnp.dot(normed[...], flat, preferred_element_type=jnp.float32).astype(jnp.bfloat16)
         attend(g, 1 - core, mixed_out)
@@ -439,9 +442,7 @@
             out_copy(n - 2, slot).wait()
         proj = jnp.dot(mixed_own[...], w_cols[slot, 0:half], preferred_element_type=jnp.float32)
         proj = proj + jnp.dot(mixed_in[...], w_cols[slot, half:2 * half], preferred_element_type=jnp.float32)
-        proj = proj.astype(jnp.bfloat16).astype(jnp.float32)
-        cols = pl.ds(pl.multiple_of(n * tile, tile), tile)
-        out_tile[slot] = (y_in[:, cols].astype(jnp.float32) + proj).astype(jnp.bfloat16)
+        out_tile[slot] = proj.astype(jnp.bfloat16)
         out_copy(n, slot).start()
 
         @pl.when(n + 2 < tiles)
@@ -455,8 +456,8 @@
         mixed_copy(g).wait_send()
 
 
-def attention_stage(seq_len, normed, incoming, w_query, w_key, w_value, w_out):
-    tokens, dim = incoming.shape
+def attention_stage(seq_len, normed, w_query, w_key, w_value, w_out):
+    _, tokens, dim = normed.shape
     heads, head_dim = w_query.shape[1:]
     group = 8
     tile = 1024
@@ -467,48 +468,41 @@
     return pl.pallas_call(
         functools.partial(attention_kernel, seq_len),
         out_shape=jax.ShapeDtypeStruct((tokens, dim), bf16),
-        in_specs=[hbm] * 6,
+        in_specs=[hbm] * 5,
         out_specs=hbm,
         scratch_shapes=[
-            pltpu.VMEM((tokens, dim), bf16), pltpu.VMEM((2 * tokens, dim), bf16),
+            pltpu.VMEM((2 * tokens, dim), bf16),
             pltpu.VMEM((3, dim, group, head_dim), bf16), pltpu.VMEM((2, heads * head_dim, tile), bf16),
             pltpu.VMEM((3, 2 * tokens, group * head_dim), bf16),
             pltpu.VMEM((tokens, half), bf16), pltpu.VMEM((tokens, half), bf16), pltpu.VMEM((tokens, half), bf16),
             pltpu.VMEM((2, tokens, tile), bf16),
-            dma((2,)), dma(()), dma((3,)), dma((2, 2)), dma((2,)), dma((heads // group // 2,)), dma((heads // group // 2,)),
+            dma((2,)), dma((3,)), dma((2, 2)), dma((2,)), dma((heads // group // 2,)), dma((heads // group // 2,)),
         ],
         compiler_params=pltpu.CompilerParams(
             collective_id=1, has_side_effects=True, vmem_limit_bytes=67_000_000),
         name="attention_stage",
-    )(normed, incoming, w_query, w_key, w_value, w_out.reshape(heads * head_dim, dim))
+    )(normed, w_query, w_key, w_value, w_out.reshape(heads * head_dim, dim))
 
 
 def solution(mesh):
-    ep_size = mesh.shape["ep"]
     tok_spec = P("pp", "data", "ep", None, None)
     vec_spec = P("pp", None)
     mat_spec = P("pp", None, None)
     head_spec = P("pp", None, None, None)
 
     def device_step(expert_out, expert_ids, slot_ids, gate_weights, residual, norm_moe, w_gate, w_up, w_down, norm_attn, w_query, w_key, w_value, w_out):
-        seqs, seq_len, top_k = expert_ids.shape[2:]
+        seqs, seq_len = expert_ids.shape[2:4]
         tokens = seqs * seq_len
         dim = residual.shape[-1]
-        cap_slots = expert_out.shape[3] // ep_size
-        first_slot = lax.axis_index("ep") * cap_slots
 
         def choices_first(array):
             return jnp.swapaxes(array[0, 0], 1, 2)
 
-        slot_here = choices_first(slot_ids)
-        kept_mask = slot_here >= 0
-        col_ids = jnp.where(kept_mask, choices_first(expert_ids) * cap_slots + slot_here - first_slot, -1)
-        weights = jnp.where(kept_mask, choices_first(gate_weights), 0.0)
-        meta = jnp.concatenate([col_ids.astype(jnp.float32), weights], axis=1)
-        meta = jnp.pad(meta, ((0, 0), (0, 0), (0, 128 - seq_len)))
         normed, incoming = combine_stage(
-            meta, expert_out[0, 0], residual.reshape(tokens, dim), norm_moe, norm_attn, w_gate[0], w_up[0], w_down[0])
-        result = attention_stage(seq_len, normed, incoming, w_query[0], w_key[0], w_value[0], w_out[0])
+            choices_first(expert_ids), choices_first(slot_ids), choices_first(gate_weights), expert_out[0, 0],
+            residual.reshape(tokens, dim), norm_moe, norm_attn, w_gate[0], w_up[0], w_down[0])
+        projected = attention_stage(seq_len, normed, w_query[0], w_key[0], w_value[0], w_out[0])
+        result = (incoming.astype(jnp.float32) + projected.astype(jnp.float32)).astype(jnp.bfloat16)
         return result.reshape(1, 1, seqs, seq_len, dim)
 
     in_specs = (tok_spec,) * 5 + (vec_spec, mat_spec, mat_spec, mat_spec, vec_spec, head_spec, head_spec, head_spec, head_spec)

time: 137 us -> 132 us (0.964)
  Pallas kernels: 132 us -> 129 us
  local copies, waits for them, and re-layouts: 2.7 us -> 0 us
  other arithmetic: 2.07 us -> 3.57 us
    pallas_call x1, Pallas kernels: 43.1 us -> 40.2 us  [attention_stage(): pl.pallas_call(functools.partial(attention_kernel, seq_len), out_shape=ja...]
    convert_element_type x1, other arithmetic: 0.73 us -> 3.57 us  [device_step(): (incoming.astype(jnp.float32) + projected.astype(jnp.float32)).astype(jnp...]
    unnamed x1 -> x0, local copies, waits for them, and re-layouts: 2.7 us -> none
where the time goes in v5:
time: 132 us
  Pallas kernels  129 us (98%)
  other arithmetic  3.57 us (3%)
    pallas_call x1, Pallas kernels, combine_stage(): pl.pallas_call(combine_kernel, out_shape=(jax.ShapeDtypeStruct((2,) + ful...  88.4 us
    pallas_call x1, Pallas kernels, attention_stage(): pl.pallas_call(functools.partial(attention_kernel, seq_len), out_shape=ja...  40.2 us
    convert_element_type x1, other arithmetic, device_step(): (incoming.astype(jnp.float32) + projected.astype(jnp.float32)).astype(jnp...  3.57 us

profile of v5, /device:TPU:0, one launch (start us, length us, event | category | flops | bytes accessed | tf_op | source)
XLA Modules:
  0.0 132.2 jit_solution(16830864943695272298)
XLA Ops:
  0.0 88.4 %combine_stage.1 = (bf16[2,192,4096]{2,1,0:T(8,128)(2,1)}, bf16[192,4096]{1,0:T(8,128)(2,1)}) custom-call(s32[3,8,64]{2,1,0:T(8,128)} %bitcast.28, s32[3,8,64]{2,1,0:T(8,128)} %bitcast.29, f32[3,8,64]{2,1,0:T(8,128)} %bitcast.30, bf16[64,32,4096]{2,1,0:T(8,128)(2,1)} %bitcast.23, bf16[192,4096]{1,0:T(8,128)(2,1)} %bitcast.27, f32[1,4096]{1,0:T(1,128)} %norm_ref.1, ...), custom_call_target="tpu_custom_call" | custom-call | tf_op jit(solution)/shard_map/combine_stage/pallas_call | solution.py:306
  88.4 40.2 %attention_stage.1 = bf16[192,4096]{1,0:T(8,128)(2,1)} custom-call(bf16[2,192,4096]{2,1,0:T(8,128)(2,1)} %get-tuple-element.8.x_hbm, bf16[4096,32,128]{2,1,0:T(8,128)(2,1)} %bitcast.19, bf16[4096,32,128]{2,1,0:T(8,128)(2,1)} %bitcast.20, bf16[4096,32,128]{2,1,0:T(8,128)(2,1)} %bitcast.21, bf16[4096,4096]{1,0:T(8,128)(2,1)} %bitcast.22), custom_call_target="tpu_custom_call" | custom-call | tf_op jit(solution)/shard_map/attention_stage/pallas_call | solution.py:468
  128.6 3.6 %add_convert_fusion = bf16[192,4096]{1,0:T(8,128)(2,1)} fusion(bf16[192,4096]{1,0:T(8,128)(2,1)} %attention_stage.1, bf16[192,4096]{1,0:T(8,128)(2,1)} %get-tuple-element.7), kind=kLoop, calls=%fused_computation | loop fusion | flops 3145728 | bytes 4718592 | tf_op jit(solution)/shard_map/convert_element_type | solution.py:505
